TPU v7x, 256 devices: a whole 4x4x8 slice. The times are simulated.
256 devices in a mesh: outer: 16 (over z_hi, x, core), chip: 16 (over y, z_lo).
Axes of the slice: x: 4, y: 4, z: 8 (z_hi: 2, z_lo: 4; z = z_hi * 4 + z_lo), core: 2. Of those that a mesh axis runs over, the one named last changes fastest.
Arguments:
- inputs: bfloat16 [32768, 2048], P(('outer', 'chip')), may hold values from -6 to 6
- out_grads: bfloat16 [32768, 2048], P(('outer', 'chip')), may hold values from -6 to 6
- weight: bfloat16 [2048, 2048], P('chip'), may hold values from -0.125 to 0.125
- start_basis: float32 [128, 2048], P('chip'), may hold values from -6 to 6
- error_buffer: float32 [16, 2048, 2048], P('outer', 'chip'), may hold values from -2 to 2
Outputs:
- outputs: bfloat16 [32768, 2048], P(('outer', 'chip'))
- new_error: float32 [16, 2048, 2048], P('outer', 'chip')
All inputs are finite; a program needn't handle non-finite values.
Results may differ from a plain program's by a relative error of at most 0.0085.
Values may be sent and summed in bfloat16 or wider, within the bound.
A program may use at most 128 MiB of HBM per device.

v0:
```python
import jax
import jax.numpy as jnp
from jax import lax
from jax.sharding import Mesh
from jax.sharding import PartitionSpec as P

TOK_DEV = 128
CHIP = ("chip_0", "chip_1")
OUTER_CHIP = ("outer", "chip_0", "chip_1")


LEARNING_RATE = 0.2


def summed_rows(subtotal, axes):
    for axis in axes:
        subtotal = lax.psum_scatter(subtotal, axis, scatter_dimension=0, tiled=True)
    return subtotal


def copy_for_each(shard, axis):
    length = lax.axis_size(axis)
    return lax.all_to_all(
        jnp.broadcast_to(shard[None], (length, *shard.shape)), axis, 0, 0, tiled=True
    )


def taken_together(shard, axis):
    return copy_for_each(shard, axis).sum(axis=0)


def taken_together_2(shard, axis):
    everything = copy_for_each(shard, axis)
    return jnp.sum(everything.astype(jnp.float32), axis=0)


def orthonormal(projected):
    finished = []
    for index in range(projected.shape[-2]):
        vector = projected[..., index, :]
        for unit in finished:
            vector = vector - jnp.sum(vector * unit, axis=-1, keepdims=True) * unit
        finished.append(vector / jnp.sqrt(jnp.sum(vector * vector, axis=-1, keepdims=True) + 1.0))
    return jnp.stack(finished, axis=-2)


def shards(inputs, out_grads, weight, start_basis, error_buffer):
    highest = lax.Precision.HIGHEST
    pod_count = lax.axis_size("outer")
    columns = inputs
    gradient = (
        summed_rows(
            lax.dot_general(
                columns, out_grads, (((0,), (0,)), ((), ())), preferred_element_type=jnp.float32
            ),
            CHIP,
        )
        / TOK_DEV
    )
    merged = gradient + error_buffer[0]
    projected = lax.dot_general(
        start_basis,
        merged,
        (((1,), (1,)), ((), ())),
        precision=highest,
        preferred_element_type=jnp.float32,
    )
    projected = taken_together(projected, "outer") / pod_count
    left_basis = orthonormal(projected)
    right_factor = jnp.dot(
        left_basis, merged, precision=highest, preferred_element_type=jnp.float32
    )
    right_factor = (
        taken_together_2(right_factor.astype(jnp.bfloat16), "outer").astype(jnp.float32) / pod_count
    )
    approx = lax.dot_general(
        left_basis,
        right_factor,
        (((0,), (0,)), ((), ())),
        precision=highest,
        preferred_element_type=jnp.float32,
    )
    new_error = (merged - approx)[None]
    new_weight = (weight.astype(jnp.float32) - LEARNING_RATE * approx).astype(jnp.bfloat16)
    columns = inputs
    result = jnp.dot(
        columns,
        lax.all_gather(new_weight, CHIP, axis=0, tiled=True),
        preferred_element_type=jnp.float32,
    )
    return (result.astype(jnp.bfloat16), new_error)


def solution(mesh):
    finer = Mesh(mesh.devices.reshape(mesh.shape["outer"], 4, 4), ("outer", "chip_0", "chip_1"))
    in_specs = (
        P(OUTER_CHIP, None),
        P(OUTER_CHIP, None),
        P(CHIP, None),
        P(CHIP, None),
        P("outer", CHIP, None),
    )
    out_specs = (P(OUTER_CHIP, None), P("outer", CHIP, None))
    return jax.shard_map(
        shards, mesh=finer, in_specs=in_specs, out_specs=out_specs, check_vma=False
    )
```

profile of v0, /device:TPU:1, one launch (start us, length us, event | category | flops | bytes accessed | tf_op | source)
XLA Modules:
  0.0 557.5 jit_solution(15917783229556293585)
XLA Ops:
  7.2 0.0 copy-start
  7.2 0.0 reduce-scatter.3.cloned.1.call-start
  7.2 1.0 copy-done
  8.2 9.1 %fusion.15 = f32[2048,2048]{1,0:T(8,128)} fusion(bf16[128,2048]{1,0:T(8,128)(2,1)S(1)} %copy-done, bf16[128,2048]{1,0:T(8,128)(2,1)} %param.6), kind=kOutput, calls=%fused_computation.104 | convolution fusion | flops 1073741824 | bytes 17825792 | tf_op jit(solution)/shard_map/dot_general | solution.py:53
  17.3 0.0 copy-start.1
  17.3 0.0 copy-start.3
  17.3 0.0 reduce-scatter.3.cloned.1.call-update
  17.4 0.0 copy-start.2
  17.4 0.0 reduce-scatter.5.cloned.1.call-start
  17.4 154.3 %reduce-scatter.3.cloned.1.call-done = f32[512,2048]{1,0:T(8,128)} async-done(((f32[2048,2048]{1,0:T(8,128)}), f32[512,2048]{1,0:T(8,128)}) %reduce-scatter.3.cloned.1.call-update) | async-done | bytes 4194320 | tf_op jit(solution)/shard_map/reduce_scatter | solution.py:17
  171.8 0.0 reduce-scatter.5.cloned.1.call-update
  171.8 0.0 all-gather.2.cloned.1.call-start
  171.8 83.9 %reduce-scatter.5.cloned.1.call-done = f32[128,2048]{1,0:T(8,128)} async-done(((f32[512,2048]{1,0:T(8,128)}), f32[128,2048]{1,0:T(8,128)}) %reduce-scatter.5.cloned.1.call-update) | async-done | bytes 1048592 | tf_op jit(solution)/shard_map/reduce_scatter | solution.py:17
  255.7 0.0 copy-done.1
  255.7 0.0 copy-done.3
  255.7 2.1 convolution_bitcast_fusion
  257.9 19.1 %all_to_all.10 = f32[16,8,128]{2,1,0:T(8,128)S(1)} all-to-all(f32[16,8,128]{2,1,0:T(8,128)S(1)} %broadcast_in_dim.6), channel_id=1, replica_groups=mesh['outer'=16,'chip_0'=4,'chip_1'=4] {'outer'}, dimensions={0} | all-to-all | bytes 131072 | tf_op jit(solution)/shard_map/all_to_all | solution.py:23
  277.0 0.6 multiply_reduce_fusion.28
  278.3 0.6 fusion.10
  278.9 1.3 fusion.4
  281.0 2.0 multiply_reduce_fusion.26
  283.0 4.4 multiply_reduce_fusion.6
  288.1 4.5 multiply_reduce_fusion.5
  292.5 1.9 multiply_reduce_fusion.22
  295.1 1.8 multiply_reduce_fusion.19
  297.0 5.1 multiply_reduce_fusion.4
  302.7 3.2 multiply_reduce_fusion.3
  305.9 1.8 multiply_reduce_fusion.13
  308.4 2.0 multiply_reduce_fusion.8
  310.3 2.6 multiply_reduce_fusion.2
  313.6 2.0 multiply_reduce_fusion.1
  315.6 1.9 multiply_reduce_fusion
  318.2 17.6 %subtract_divide_fusion = (f32[1,128]{1,0:T(1,128)S(1)}, f32[1,128]{1,0:T(1,128)S(1)}, f32[1,128]{1,0:T(1,128)S(1)}, f32[1,128]{1,0:T(1,128)S(1)}, f32[1,128]{1,...) fusion(f32[1,128]{1,0:T(1,128)S(1)} %get-tuple-element.67, f32[]{:T(128)S(6)} %sqrt.39, f32[]{:T(128)} %get-tuple-element.40, ...), kind=kLoop, calls=%fused_computation.41 | loop fusion | flops 8064 | bytes 7820 | tf_op jit(solution)/shard_map/div | solution.py:43
  335.7 1.9 convolution_convert_fusion.1
  337.7 18.1 %all_to_all.11 = bf16[16,8,2048]{2,1,0:T(8,128)(2,1)S(1)} all-to-all(bf16[16,8,2048]{2,1,0:T(8,128)(2,1)S(1)} %broadcast_in_dim.7), channel_id=1, replica_groups=mesh['outer'=16,'chip_0'=4,'chip_1'=4] {'outer'}, dimensions={0} | all-to-all | bytes 1048576 | tf_op jit(solution)/shard_map/all_to_all | solution.py:23
  355.8 0.1 convert_reduce_fusion
  355.9 0.0 copy-done.2
  355.9 3.5 subtract_bitcast_fusion
  359.4 0.0 all-gather.2.cloned.1.call-update
  359.4 184.7 %all-gather.2.cloned.1.call-done = bf16[2048,2048]{1,0:T(8,128)(2,1)} async-done(((bf16[128,2048]{1,0:T(8,128)(2,1)}), bf16[2048,2048]{1,0:T(8,128)(2,1)}) %all-gather.2.cloned.1.call-update) | async-done | bytes 8388624 | tf_op jit(solution)/shard_map/all_gather | solution.py:88
  544.1 5.8 %fusion = bf16[128,2048]{0,1:T(8,128)(2,1)S(1)} fusion(bf16[2048,2048]{1,0:T(8,128)(2,1)} %all-gather.2.cloned.1.call-done, bf16[128,2048]{1,0:T(8,128)(2,1)S(1)} %copy-done), kind=kOutput, calls=%fused_computation.1 | convolution fusion | flops 1074003968 | bytes 9437184 | tf_op jit(solution)/shard_map/dot_general | solution.py:86
  549.9 1.0 copy.8
  (5 shorter events, 0.1 us)
Async XLA Ops:
  7.2 1.0 copy-start
  7.2 164.6 %reduce-scatter.3.cloned.1.call-start = ((), (), s32[]{:S(2)}) async-start(), calls=%async_computation.4 | async-start | bytes 20971520 | tf_op jit(solution)/shard_map/reduce_scatter | solution.py:17
  17.3 238.4 %copy-start.1 = (f32[1,128,2048]{2,1,0:T(8,128)S(1)}, f32[1,128,2048]{2,1,0:T(8,128)}, u32[]{:S(2)}) copy-start(f32[1,128,2048]{2,1,0:T(8,128)} %param.9) | copy-start | bytes 3145732
  17.3 238.4 %copy-start.3 = (f32[8,2048]{1,0:T(8,128)S(1)}, f32[8,2048]{1,0:T(8,128)}, u32[]{:S(2)}) copy-start(f32[8,2048]{1,0:T(8,128)} %param.8) | copy-start | bytes 196612
  17.4 338.5 %copy-start.2 = (bf16[128,2048]{1,0:T(8,128)(2,1)S(1)}, bf16[128,2048]{1,0:T(8,128)(2,1)}, u32[]{:S(2)}) copy-start(bf16[128,2048]{1,0:T(8,128)(2,1)} %param.7) | copy-start | bytes 1572868
  17.4 238.3 %reduce-scatter.5.cloned.1.call-start = ((), (), s32[]{:S(2)}) async-start(), calls=%async_computation.5 | async-start | bytes 5242880 | tf_op jit(solution)/shard_map/reduce_scatter | solution.py:17
  171.8 372.4 %all-gather.2.cloned.1.call-start = ((), (), s32[]{:S(2)}) async-start(), calls=%async_computation.6 | async-start | bytes 8912896 | tf_op jit(solution)/shard_map/all_gather | solution.py:88
Sparse Core Ops, SparseCore 0:
  17.5 154.2 reduce-scatter.2
  174.3 81.3 reduce-scatter.4
  359.6 184.5 all-gather.1
where the time goes:
time: 559 us; the launch traced here: 557 us
  waiting for transfers between devices  423 us (76%)
  other arithmetic  53.3 us (10%)
  blocking collectives  37.2 us (7%)
  matrix products  22.5 us (4%)
  between operations  19.3 us (3%)
    reduce_scatter x2, waiting for transfers between devices, summed_rows(): subtotal = lax.psum_scatter(subtotal, axis, scatter_dimension=0, tiled=True)  238 us
    all_gather x1, waiting for transfers between devices, shards(): lax.all_gather(new_weight, CHIP, axis=0, tiled=True)  185 us
    all_to_all x2, blocking collectives, copy_for_each(): lax.all_to_all(jnp.broadcast_to(shard[None], (length, *shard.shape)), axi...  37.2 us
    reduce_sum x11, other arithmetic, orthonormal(): vector = vector - jnp.sum(vector * unit, axis=-1, keepdims=True) * unit  29.4 us
    div x1, other arithmetic, orthonormal(): vector / jnp.sqrt(jnp.sum(vector * vector, axis=-1, keepdims=True) + 1.0)  17.6 us
  transfers between devices with their start and end apart: 3, of which 3 were waited for; matrix products, arithmetic and copies ran while one was open for 0% of the time, Pallas kernels for 0%

commit v1 on v0

v1 whole, which is shorter than its diff:
```python
import jax
import jax.numpy as jnp
from jax import lax
from jax.experimental import pallas as pl
from jax.experimental.pallas import tpu as pltpu
from jax.sharding import Mesh
from jax.sharding import PartitionSpec as P

MESH_ID = pl.DeviceIdType.MESH
AXES = ("zh", "x", "core", "y", "z")
LEARNING_RATE = 0.2
TOK = 128
D = 2048
NCH = 8
CW = D // NCH
F32 = jnp.float32
BF16 = jnp.bfloat16


def body(
    x_hbm, g_hbm, w_hbm, b_hbm, e_hbm, out_hbm, ne_hbm,
    xx, xp, xgt, dyb, wg, eb, bb, pf, sb, rl, rr, mg, xo, xw, lf, lall, rt, rsb, rall, ob,
    ld_x, ld_g, ld_w, ld_b, ld_e,
    wz_s, wz_r, wy_s, wy_r, wc_s, wc_r, xp_s, xp_r, xx_s, xx_r,
    dy_s, dy_r, re_s, re_r, rs_s, rsl_r, rsr_r,
    lf_s, lf_r, la_s, la_r, rt_s, rt_r, ro_s, ro_r, rc_s, rc_r, xo_s, xo_r,
    ne_s, out_s,
):
    zh, x, core, y, z = (lax.axis_index(a) for a in AXES)
    outer = (zh * 4 + x) * 2 + core
    sl = x * 2 + core
    c = y * 4 + z

    def remote(src, dst, ssem, rsem, dev):
        return pltpu.make_async_remote_copy(
            src_ref=src, dst_ref=dst, send_sem=ssem, recv_sem=rsem,
            device_id=dev, device_id_type=MESH_ID,
        )

    def outer_dev(o):
        return {"zh": o // 8, "x": (o // 2) % 4, "core": o % 2}

    def chip_dev(k):
        return {"y": k // 4, "z": k % 4}

    yp, ym = (y + 1) % 4, (y + 3) % 4
    y2 = (y + 2) % 4

    w_ld = pltpu.make_async_copy(w_hbm.at[:, pl.ds(pl.multiple_of(sl * CW, CW), CW)], wg.at[core, y, z], ld_w.at[0])
    w_ld.start()
    x_ld = [pltpu.make_async_copy(x_hbm.at[:, pl.ds(q * 512, 512)], xx.at[x, q], ld_x.at[q]) for q in range(4)]
    for cp in x_ld:
        cp.start()
    g_ld = [pltpu.make_async_copy(g_hbm.at[:, pl.ds(n * CW, CW)], dyb.at[n, y], ld_g.at[n]) for n in range(NCH)]
    for cp in g_ld:
        cp.start()
    b_ld = [pltpu.make_async_copy(b_hbm.at[:, pl.ds(n * CW, CW)], bb.at[n], ld_b.at[n]) for n in range(NCH)]
    e_ld = [pltpu.make_async_copy(e_hbm.at[0, :, pl.ds(n * CW, CW)], eb.at[n], ld_e.at[n]) for n in range(NCH)]
    for cp in b_ld + e_ld:
        cp.start()

    barrier = pltpu.get_barrier_semaphore()

    @pl.loop(1, 16)
    def _(i):
        pl.semaphore_signal(barrier, inc=1, device_id=outer_dev((outer + i) % 16), device_id_type=MESH_ID)
        pl.semaphore_signal(barrier, inc=1, device_id=chip_dev((c + i) % 16), device_id_type=MESH_ID)

    pl.semaphore_wait(barrier, 30)

    def wz_copy(p):
        return remote(wg.at[core, y, z], wg.at[core, y, z], wz_s.at[p], wz_r.at[z], {"z": p})

    def wz_recv(p):
        return remote(wg.at[core, y, p], wg.at[core, y, p], wz_s.at[p], wz_r.at[p], {"z": p})

    def wy_copy(p):
        return remote(wg.at[core, y], wg.at[core, y], wy_s.at[p], wy_r.at[y], {"y": p})

    def wy_recv(p):
        return remote(wg.at[core, p], wg.at[core, p], wy_s.at[p], wy_r.at[p], {"y": p})

    def wc_copy():
        return remote(wg.at[core], wg.at[core], wc_s.at[0], wc_r.at[0], {"core": 1 - core})

    def wc_recv():
        return remote(wg.at[1 - core], wg.at[1 - core], wc_s.at[0], wc_r.at[0], {"core": 1 - core})

    def xp_copy(p):
        return remote(xx.at[x, p], xp.at[y], xp_s.at[p], xp_r.at[y], {"y": p})

    def xp_recv(p):
        return remote(xx.at[x, p], xp.at[p], xp_s.at[p], xp_r.at[p], {"y": p})

    def xx_copy(p):
        return remote(xx.at[x], xx.at[x], xx_s.at[p], xx_r.at[x], {"x": p})

    def xx_recv(p):
        return remote(xx.at[p], xx.at[p], xx_s.at[p], xx_r.at[p], {"x": p})

    def dy_copy(d, n):
        return remote(dyb.at[n, y], dyb.at[n, y], dy_s.at[d, n], dy_r.at[d, n], {"y": yp if d == 0 else ym})

    def dy_recv(d, n):
        src = ym if d == 0 else yp
        return remote(dyb.at[n, src], dyb.at[n, src], dy_s.at[d, n], dy_r.at[d, n], {"y": yp})

    def relay(n, up):
        blk = ym if up else yp
        return remote(dyb.at[n, blk], dyb.at[n, blk], re_s.at[n], re_r.at[n], {"y": yp if up else ym})

    def relay_recv(n):
        return remote(dyb.at[n, y2], dyb.at[n, y2], re_s.at[n], re_r.at[n], {"y": yp})

    def do_relay(n):
        for d in range(2):
            dy_recv(d, n).wait_recv()

        @pl.when(n % 2 == 0)
        def _():
            relay(n, True).start()

        @pl.when(n % 2 == 1)
        def _():
            relay(n, False).start()

    w_ld.wait()
    for i in range(1, 4):
        wz_copy((z + i) % 4).start()
    for cp in x_ld:
        cp.wait()
    for i in (1, 3, 2):
        xp_copy((y + i) % 4).start()
    for n in range(NCH):
        g_ld[n].wait()
        for d in range(2):
            dy_copy(d, n).start()
    for i in (1, 3, 2):
        xx_copy((x + i) % 4).start()
    for cp in b_ld + e_ld:
        cp.wait()

    for i in range(4):
        @pl.when(y == i)
        def _():
            xgt[:, pl.ds(i * TOK, TOK)] = xx[x, i].T

        @pl.when(y != i)
        def _():
            xp_recv(i).wait_recv()
            xgt[:, pl.ds(i * TOK, TOK)] = xp[i].T

    do_relay(0)
    do_relay(1)

    lf[outer] = jnp.zeros((8, TOK), F32)

    @pl.loop(0, NCH + 3)
    def _(s):
        @pl.when(s + 2 < NCH)
        def _():
            do_relay(s + 2)

        @pl.when(s == 2)
        def _():
            for i in range(1, 4):
                wz_recv((z + i) % 4).wait_recv()
            for i in (1, 3, 2):
                wy_copy((y + i) % 4).start()

        @pl.when(s == 7)
        def _():
            for i in range(1, 4):
                wy_recv((y + i) % 4).wait_recv()
            wc_copy().start()

        @pl.when(s < NCH)
        def _():
            relay_recv(s).wait_recv()
            part = jnp.dot(xgt[...], dyb[s].reshape(512, CW), preferred_element_type=F32)
            pf[s] = part.reshape(4, TOK, CW)

        jr = s - z
        jl = s - (3 - z)
        for d in (3, 2, 1):
            @pl.when((jr >= 0) & (jr < NCH) & (d > z))
            def _():
                cp = remote(sb.at[jr, d], rl.at[jr, d], rs_s.at[jr, d], rsl_r.at[jr, d], {"z": (z + 1) % 4})

                @pl.when(z == 0)
                def _():
                    sb[jr, d] = pf[jr, d].astype(BF16)

                @pl.when(z > 0)
                def _():
                    cp.wait_recv()
                    sb[jr, d] = (pf[jr, d] + rl[jr, d].astype(F32)).astype(BF16)

                cp.start()
        for d in (0, 1, 2):
            @pl.when((jl >= 0) & (jl < NCH) & (d < z))
            def _():
                cp = remote(sb.at[jl, d], rr.at[jl, d], rs_s.at[jl, d], rsr_r.at[jl, d], {"z": (z + 3) % 4})

                @pl.when(z == 3)
                def _():
                    sb[jl, d] = pf[jl, d].astype(BF16)

                @pl.when(z < 3)
                def _():
                    cp.wait_recv()
                    sb[jl, d] = (pf[jl, d] + rr[jl, d].astype(F32)).astype(BF16)

                cp.start()

        @pl.when(s >= 3)
        def _():
            n = s - 3
            mg[n] = pf[n, z]

            @pl.when(z > 0)
            def _():
                remote(sb.at[n, z], rl.at[n, z], rs_s.at[n, z], rsl_r.at[n, z], {"z": (z + 1) % 4}).wait_recv()
                mg[n] = mg[n] + rl[n, z].astype(F32)

            @pl.when(z < 3)
            def _():
                remote(sb.at[n, z], rr.at[n, z], rs_s.at[n, z], rsr_r.at[n, z], {"z": (z + 3) % 4}).wait_recv()
                mg[n] = mg[n] + rr[n, z].astype(F32)

            m = mg[n] * (1.0 / TOK) + eb[n]
            mg[n] = m
            lf[outer] = lf[outer] + lax.dot_general(
                bb[n], m, (((1,), (1,)), ((), ())), precision=lax.Precision.HIGHEST, preferred_element_type=F32
            )

    def lf_copy(o, own):
        return remote(lf.at[own], lf.at[own], lf_s.at[o], lf_r.at[own], outer_dev(o))

    @pl.loop(1, 16)
    def _(i):
        lf_copy((outer + i) % 16, outer).start()

    for i in range(1, 4):
        xx_recv((x + i) % 4).wait_recv()
    wc_recv().wait_recv()
    for h in range(2):
        acc = jnp.zeros((512, CW), F32)
        for q in range(4):
            acc = acc + jnp.dot(
                xx[:, q].reshape(512, 512), wg[h, q].reshape(512, CW), preferred_element_type=F32
            )
        xo[:, h] = acc.reshape(4, TOK, CW).astype(BF16)

    def xo_copy(p):
        return remote(xo.at[p], xw.at[x], xo_s.at[p], xo_r.at[x], {"x": p})

    def xo_recv(p):
        return remote(xo.at[p], xw.at[p], xo_s.at[p], xo_r.at[p], {"x": p})

    for i in (1, 3, 2):
        xo_copy((x + i) % 4).start()
    xw[x] = xo[x]

    @pl.loop(1, 16)
    def _(i):
        p = (outer + i) % 16
        lf_copy(p, p).wait_recv()

    v = jnp.sum(lf[...], axis=0) * (1.0 / 16)
    rows = lax.broadcasted_iota(jnp.int32, (8, TOK), 0)
    for k in range(8):
        row = v[k:k + 1]
        dots = jnp.sum(v * row, axis=-1, keepdims=True)
        norm = jnp.sqrt(dots[k:k + 1] + 1.0)
        unit = row / norm
        v = jnp.where(rows > k, v - (dots / norm) * unit, jnp.where(rows == k, unit, v))
    lall[c] = v

    def la_copy(p, own):
        return remote(lall.at[own], lall.at[own], la_s.at[p], la_r.at[own], chip_dev(p))

    vh = v.astype(BF16)
    for n in range(NCH):
        rt[n] = jnp.dot(vh, mg[n].astype(BF16), preferred_element_type=F32).astype(BF16)

    def rt_copy(o):
        return remote(rt.at[o % 8], rsb.at[outer], rt_s.at[o], rt_r.at[outer], outer_dev(o))

    def rt_recv(o):
        return remote(rt.at[o % 8], rsb.at[o], rt_s.at[o], rt_r.at[o], outer_dev(o))

    @pl.loop(1, 16)
    def _(i):
        rt_copy((outer + i) % 16).start()

    rsb[outer] = rt[sl]

    @pl.loop(1, 16)
    def _(i):
        la_copy((c + i) % 16, c).start()

    @pl.loop(1, 16)
    def _(i):
        rt_recv((outer + i) % 16).wait_recv()

    rall[c, sl] = (jnp.sum(rsb[...].astype(F32), axis=0) * (1.0 / 16)).astype(BF16)

    def ro_copy(t, own):
        return remote(rall.at[c, own], rall.at[c, own], ro_s.at[t], ro_r.at[own], {"x": t // 2, "core": t % 2})

    @pl.loop(1, 8)
    def _(i):
        ro_copy((sl + i) % 8, sl).start()

    @pl.loop(1, 16)
    def _(i):
        p = (c + i) % 16
        la_copy(p, p).wait_recv()

    lmat = lall[...].reshape(TOK, TOK)
    lrow = lax.broadcasted_iota(jnp.int32, (TOK, TOK), 0) // 8
    t = jnp.zeros((TOK, TOK), F32)
    for q in range(4):
        lq = jnp.concatenate(
            [jnp.where(lrow == q * 4 + j, lmat, 0.0).astype(BF16) for j in range(4)], axis=1
        )
        t = t + lax.dot_general(xx[x, q], lq, (((1,), (1,)), ((), ())), preferred_element_type=F32)
    t = (t * (-LEARNING_RATE)).astype(BF16)

    @pl.loop(1, 8)
    def _(i):
        p = (sl + i) % 8
        ro_copy(p, p).wait_recv()

    def rc_copy(p, own):
        return remote(rall.at[own], rall.at[own], rc_s.at[p], rc_r.at[own], chip_dev(p))

    @pl.loop(1, 16)
    def _(i):
        rc_copy((c + i) % 16, c).start()

    vt = v.T
    vt_hi = vt.astype(BF16)
    vt_lo = (vt - vt_hi.astype(F32)).astype(BF16)
    for n in range(NCH):
        rn = rall[c, n]
        approx = jnp.dot(vt_hi, rn, preferred_element_type=F32) + jnp.dot(vt_lo, rn, preferred_element_type=F32)
        mg[n] = mg[n] - approx
        pltpu.make_async_copy(mg.at[n], ne_hbm.at[0, :, pl.ds(n * CW, CW)], ne_s.at[n]).start()

    for i in range(1, 4):
        xo_recv((x + i) % 4).wait_recv()

    @pl.loop(1, 16)
    def _(i):
        p = (c + i) % 16
        rc_copy(p, p).wait_recv()

    for n in range(NCH):
        rn = rall[:, n].astype(F32).reshape(TOK, CW).astype(BF16)
        ob[n] = (xw[n // 2, n % 2].astype(F32) + jnp.dot(t, rn, preferred_element_type=F32)).astype(BF16)
        pltpu.make_async_copy(ob.at[n], out_hbm.at[:, pl.ds(n * CW, CW)], out_s.at[n]).start()

    for i in range(1, 4):
        wz_copy((z + i) % 4).wait_send()
        wy_copy((y + i) % 4).wait_send()
        xp_copy((y + i) % 4).wait_send()
        xx_copy((x + i) % 4).wait_send()
        xo_copy((x + i) % 4).wait_send()
    wc_copy().wait_send()

    @pl.loop(0, NCH)
    def _(n):
        dy_copy(0, n).wait_send()
        dy_copy(1, n).wait_send()
        relay(n, True).wait_send()
        for d in range(4):
            @pl.when(d != z)
            def _():
                remote(sb.at[n, d], rl.at[n, d], rs_s.at[n, d], rsl_r.at[n, d], {"z": (z + 1) % 4}).wait_send()

    @pl.loop(1, 16)
    def _(i):
        lf_copy((outer + i) % 16, outer).wait_send()
        rt_copy((outer + i) % 16).wait_send()
        la_copy((c + i) % 16, c).wait_send()
        rc_copy((c + i) % 16, c).wait_send()

    @pl.loop(1, 8)
    def _(i):
        ro_copy((sl + i) % 8, sl).wait_send()

    for n in range(NCH):
        pltpu.make_async_copy(mg.at[n], ne_hbm.at[0, :, pl.ds(n * CW, CW)], ne_s.at[n]).wait()
        pltpu.make_async_copy(ob.at[n], out_hbm.at[:, pl.ds(n * CW, CW)], out_s.at[n]).wait()


def step(inputs, out_grads, weight, start_basis, error_buffer):
    vm = pltpu.VMEM
    dma = pltpu.SemaphoreType.DMA
    return pl.pallas_call(
        body,
        out_shape=(
            jax.ShapeDtypeStruct((TOK, D), BF16),
            jax.ShapeDtypeStruct((1, TOK, D), F32),
        ),
        in_specs=[pl.BlockSpec(memory_space=pl.ANY)] * 5,
        out_specs=(pl.BlockSpec(memory_space=pl.ANY),) * 2,
        scratch_shapes=[
            vm((4, 4, TOK, 512), BF16),
            vm((4, TOK, 512), BF16),
            vm((512, 512), BF16),
            vm((NCH, 4, TOK, CW), BF16),
            vm((2, 4, 4, TOK, CW), BF16),
            vm((NCH, TOK, CW), F32),
            vm((NCH, 8, CW), F32),
            vm((NCH, 4, TOK, CW), F32),
            vm((NCH, 4, TOK, CW), BF16),
            vm((NCH, 4, TOK, CW), BF16),
            vm((NCH, 4, TOK, CW), BF16),
            vm((NCH, TOK, CW), F32),
            vm((4, 2, TOK, CW), BF16),
            vm((4, 2, TOK, CW), BF16),
            vm((16, 8, TOK), F32),
            vm((16, 8, TOK), F32),
            vm((NCH, 8, CW), BF16),
            vm((16, 8, CW), BF16),
            vm((16, NCH, 8, CW), BF16),
            vm((NCH, TOK, CW), BF16),
            dma((4,)), dma((NCH,)), dma((1,)), dma((NCH,)), dma((NCH,)),
            dma((4,)), dma((4,)), dma((4,)), dma((4,)), dma((1,)), dma((1,)),
            dma((4,)), dma((4,)), dma((4,)), dma((4,)),
            dma((2, NCH)), dma((2, NCH)), dma((NCH,)), dma((NCH,)),
            dma((NCH, 4)), dma((NCH, 4)), dma((NCH, 4)),
            dma((16,)), dma((16,)), dma((16,)), dma((16,)), dma((16,)), dma((16,)),
            dma((8,)), dma((8,)), dma((16,)), dma((16,)), dma((4,)), dma((4,)),
            dma((NCH,)), dma((NCH,)),
        ],
        compiler_params=pltpu.CompilerParams(
            collective_id=0, has_side_effects=True, vmem_limit_bytes=60 * 1024 * 1024
        ),
    )(inputs, out_grads, weight, start_basis, error_buffer)


def solution(mesh):
    finer = Mesh(mesh.devices.reshape(2, 4, 2, 4, 4), AXES)
    outer = ("zh", "x", "core")
    chip = ("y", "z")
    in_specs = (
        P(outer + chip, None),
        P(outer + chip, None),
        P(chip, None),
        P(chip, None),
        P(outer, chip, None),
    )
    out_specs = (P(outer + chip, None), P(outer, chip, None))
    return jax.shard_map(step, mesh=finer, in_specs=in_specs, out_specs=out_specs, check_vma=False)
```

time: 559 us -> 108 us (0.19)
  waiting for transfers between devices: 423 us -> 0 us
  Pallas kernels: 0 us -> 105 us
  other arithmetic: 53.3 us -> 0 us
  blocking collectives: 37.2 us -> 0 us
  matrix products: 22.5 us -> 0 us
  between operations: 19.3 us -> 0.65 us
    reduce_scatter x2 -> x0, waiting for transfers between devices: 238 us -> none  [summed_rows(): subtotal = lax.psum_scatter(subtotal, axis, scatter_dimension=0, tiled=True)]
    all_gather x1 -> x0, waiting for transfers between devices: 185 us -> none  [shards(): lax.all_gather(new_weight, CHIP, axis=0, tiled=True)]
    pallas_call x0 -> x1, Pallas kernels: none -> 105 us  [step(): pl.pallas_call(body, out_shape=(jax.ShapeDtypeStruct((TOK, D), BF16), jax...]
    all_to_all x2 -> x0, blocking collectives: 37.2 us -> none  [copy_for_each(): lax.all_to_all(jnp.broadcast_to(shard[None], (length, *shard.shape)), axi...]
    reduce_sum x17 -> x0, other arithmetic: 35.7 us -> none  [the longest x11 29.4 us: orthonormal(): vector = vector - jnp.sum(vector * unit, axis=-1, keepdims=True) * unit]
    dot_general x5 -> x0, matrix products: 22.5 us -> none  [the longest x1 9.13 us: shards(): lax.dot_general(columns, out_grads, (((0,), (0,)), ((), ())), preferred_e...]
    div x2 -> x0, other arithmetic: 17.6 us -> none  [the longest x1 17.6 us: orthonormal(): vector / jnp.sqrt(jnp.sum(vector * vector, axis=-1, keepdims=True) + 1.0)]
  transfers between devices with their start and end apart: 3 -> 0, of which waited for: 3 -> 0; matrix products, arithmetic and copies ran while one was open for 0% -> 0% of each run, Pallas kernels for 0% -> 0%
where the time goes in v1:
time: 108 us
  Pallas kernels  105 us (97%)
  local copies, waits for them, and re-layouts  2.94 us (3%)
    pallas_call x1, Pallas kernels, step(): pl.pallas_call(body, out_shape=(jax.ShapeDtypeStruct((TOK, D), BF16), jax...  105 us
    unnamed x4, local copies, waits for them, and re-layouts  2.94 us

profile of v1, /device:TPU:1, one launch (start us, length us, event | category | flops | bytes accessed | tf_op | source)
XLA Modules:
  0.0 108.2 jit_solution(5441185586076283308)
XLA Ops:
  0.6 104.6 %shard_map.68 = (bf16[128,2048]{1,0:T(8,128)(2,1)}, f32[1,128,2048]{2,1,0:T(8,128)}) custom-call(bf16[128,2048]{1,0:T(8,128)(2,1)} %x_hbm.1, bf16[128,2048]{1,0:T(8,128)(2,1)} %g_hbm.1, bf16[128,2048]{1,0:T(8,128)(2,1)} %w_hbm.1, f32[8,2048]{1,0:T(8,128)} %b_hbm.1, f32[1,128,2048]{2,1,0:T(8,128)} %e_hbm.1), custom_call_target="tpu_custom_call" | custom-call | tf_op jit(solution)/shard_map/pallas_call | solution.py:402
  105.2 0.0 copy-start
  105.2 2.0 %copy.9 = bf16[128,2048]{1,0:T(8,128)(2,1)} copy(bf16[128,2048]{1,0:T(8,128)(2,1)} %get-tuple-element.4) | data formatting | bytes 1048576
  107.2 0.0 copy-done
  107.2 1.0 copy.10
Async XLA Ops:
  105.2 2.0 %copy-start = (f32[1,128,2048]{2,1,0:T(8,128)S(1)}, f32[1,128,2048]{2,1,0:T(8,128)}, u32[]{:S(2)}) copy-start(f32[1,128,2048]{2,1,0:T(8,128)} %get-tuple-element.5) | copy-start | bytes 3145732

commit v2 on v0

v2 whole, which is shorter than its diff:
```python
import jax
import jax.numpy as jnp
from jax import lax
from jax.experimental import pallas as pl
from jax.experimental.pallas import tpu as pltpu
from jax.sharding import Mesh
from jax.sharding import PartitionSpec as P

MESH_ID = pl.DeviceIdType.MESH
AXES = ("zh", "x", "core", "y", "z")
LEARNING_RATE = 0.2
TOK = 128
D = 2048
NC = 16
CW = D // NC
NS = 8
SW = D // NS
LAG = 2
WZ, WD, WR, WC, XP, XR, XF, XX, DY, RE, RS, LF, LA, RT, RO, RC, RD, XO, NE, OUT = range(20)
XR2, RO2 = 18, 19
OUTER_PEERS = [(h, i, k) for h in (1, 0) for i in (2, 1, 3, 0) for k in (0, 1) if (h, i, k) != (0, 0, 0)]
CHIP_PEERS = [(j, k) for j in (2, 1, 3, 0) for k in (3, 1, 2, 0) if (j, k) != (0, 0)]
F32 = jnp.float32
BF16 = jnp.bfloat16


def body(
    x_hbm, g_hbm, w_hbm, b_hbm, e_hbm, out_hbm, ne_hbm,
    xx, xp, xr, xgt, dyb, wy, wo, eb, bb, pf, sb, rl, rr, mg, xo, xw, lf, lall, rt, rsb, rall, ob,
    ld, snd, got, xp_r, wd_r, dy_r, re_r, rs_r, rz_r, rc_r,
):
    zh, x, core, y, z = (lax.axis_index(a) for a in AXES)
    outer = (zh * 4 + x) * 2 + core
    sl = x * 2 + core
    c = y * 4 + z

    def remote(src, dst, ssem, rsem, dev):
        return pltpu.make_async_remote_copy(
            src_ref=src, dst_ref=dst, send_sem=ssem, recv_sem=rsem,
            device_id=dev, device_id_type=MESH_ID,
        )

    def outer_dev(o):
        return {"zh": (zh + o[0]) % 2, "x": (x + o[1]) % 4, "core": (core + o[2]) % 2}

    def outer_at(o):
        dev = outer_dev(o)
        return (dev["zh"] * 4 + dev["x"]) * 2 + dev["core"]

    def chip_dev(k):
        return {"y": (y + k[0]) % 4, "z": (z + k[1]) % 4}

    def chip_at(k):
        dev = chip_dev(k)
        return dev["y"] * 4 + dev["z"]

    ring = ((y + 1) % 4, (y + 3) % 4)
    y2 = (y + 2) % 4
    near = (3, 1)
    z_up, z_down = (z + 1) % 4, (z + 3) % 4

    barrier = pltpu.get_barrier_semaphore()
    for dev in OUTER_PEERS:
        pl.semaphore_signal(barrier, inc=1, device_id=outer_dev(dev), device_id_type=MESH_ID)
    for dev in CHIP_PEERS:
        pl.semaphore_signal(barrier, inc=1, device_id=chip_dev(dev), device_id_type=MESH_ID)

    w_ld = pltpu.make_async_copy(w_hbm.at[:, pl.ds(pl.multiple_of(sl * SW, SW), SW)], wy.at[z, 0], ld.at[0])
    w_ld.start()
    x_ld = [pltpu.make_async_copy(x_hbm.at[:, pl.ds(q * TOK, TOK)], xx.at[x, q], ld.at[1]) for q in range(16)]
    for q in (3, 0, 7, 4, 11, 8, 15, 12, 2, 1, 6, 5, 10, 9, 14, 13):
        x_ld[q].start()
    g_ld = [pltpu.make_async_copy(g_hbm.at[:, pl.ds(n * CW, CW)], dyb.at[n, 0], ld.at[2]) for n in range(NC)]
    for cp in g_ld:
        cp.start()
    b_ld = [pltpu.make_async_copy(b_hbm.at[:, pl.ds(n * CW, CW)], bb.at[n], ld.at[3]) for n in range(NC)]
    e_ld = [pltpu.make_async_copy(e_hbm.at[0, :, pl.ds(n * CW, CW)], eb.at[n], ld.at[4]) for n in range(NC)]
    for cp in b_ld + e_ld:
        cp.start()

    def arrived(ref, sem):
        remote(ref, ref, snd.at[0], sem, {"core": 1 - core}).wait_recv()

    def gone(ref, kind):
        remote(ref, ref, snd.at[kind], got.at[0], {"core": 1 - core}).wait_send()

    w_ld.wait()
    for i, ref in enumerate((xx.at[x], dyb.at[:, 0], bb, eb)):
        arrived(ref, ld.at[1 + i])
    with jax.named_scope("entry_barrier"):
        pl.semaphore_wait(barrier, 30)

    def wz_copy(p):
        return remote(wy.at[z, 0], wy.at[z, 0], snd.at[WZ], got.at[WZ], {"z": p})

    def wd_copy(way, j):
        return remote(wy.at[j, 0], wy.at[j, near[way]], snd.at[WD], wd_r.at[j], {"y": ring[way]})

    def wr_copy(j, way):
        return remote(wy.at[j, near[way]], wy.at[j, 2], snd.at[WR], got.at[WR], {"y": ring[way]})

    def wc_copy():
        return remote(wy, wo, snd.at[WC], got.at[WC], {"core": 1 - core})

    def xp_copy(way, d):
        p = ring[way]
        return remote(xx.at[x, p * 4 + d], xp.at[near[way], d], snd.at[XP], xp_r.at[0, int(d % 3 > 0)], {"y": p})

    def xr_copy(d):
        way = 0 if d >= 2 else 1
        return remote(xx.at[x, y2 * 4 + d], xr.at[d], snd.at[XR], got.at[XR2 if d % 3 else XR], {"y": ring[way]})

    def xf_copy(d):
        way = 0 if d >= 2 else 1
        return remote(xr.at[d], xp.at[2, d], snd.at[XF], xp_r.at[1, int(d % 3 > 0)], {"y": ring[way]})

    def xx_copy(p):
        return remote(xx.at[x], xx.at[x], snd.at[XX], got.at[XX], {"x": p})

    def dy_copy(way, n):
        return remote(dyb.at[n, 0], dyb.at[n, near[way]], snd.at[DY], dy_r.at[n], {"y": ring[way]})

    def relay(n, way):
        return remote(dyb.at[n, near[way]], dyb.at[n, 2], snd.at[RE], re_r.at[n], {"y": ring[way]})

    def direct(n):
        for way in range(2):
            dy_copy(way, n).start()

    def pass_on(n):
        with jax.named_scope("direct_wait"):
            arrived(dyb.at[n, pl.ds(0, 2)], dy_r.at[n])
        for way in range(2):
            @pl.when(n % 2 == way)
            def _():
                relay(n, way).start()

    def send_x(ds):
        for d in ds:
            for way in range(2):
                xp_copy(way, d).start()

    def pass_x(ds):
        with jax.named_scope("xr_wait"):
            arrived(xr.at[pl.ds(0, 2)], got.at[XR2 if ds[0] % 3 else XR])
        for d in ds:
            xf_copy(d).start()

    def gather_x(ds, slots):
        far = int(slots == (2,))
        if slots != (0,):
            with jax.named_scope("xp_wait"):
                arrived(xr.at[pl.ds(0, 2 if far else 4)], xp_r.at[far, int(ds[0] % 3 > 0)])
        for k in slots:
            for d in ds:
                piece = xp[k, d] if k else xx[x, y * 4 + d]
                xgt[d, :, pl.ds(k * TOK, TOK)] = piece.T

    def product(n, ds):
        block = dyb[n].reshape(4 * TOK, CW)
        for d in ds:
            pf[n, d] = jnp.dot(xgt[d], block, preferred_element_type=F32)

    def send_right(n, d):
        cp = remote(sb.at[n, d], rl.at[n, d], snd.at[RS], rs_r.at[n, d], {"z": z_up})

        @pl.when(z == 0)
        def _():
            sb[n, d] = pf[n, d].astype(BF16)

        @pl.when(z > 0)
        def _():
            with jax.named_scope("right_wait"):
                cp.wait_recv()
            sb[n, d] = (pf[n, d] + rl[n, d].astype(F32)).astype(BF16)

        cp.start()

    def send_left(n, d, h):
        def copy(sem):
            return remote(sb.at[n, d], rr.at[n, d], snd.at[RS], sem, {"z": z_down})


        @pl.when(z == 3)
        def _():
            sb[n, d] = pf[n, d].astype(BF16)

        @pl.when(z < 3)
        def _():
            with jax.named_scope("left_wait"):
                copy(rs_r.at[n, d]).wait_recv()
            sb[n, d] = (pf[n, d] + rr[n, d].astype(F32)).astype(BF16)

        if h > 1:
            copy(rs_r.at[n, d]).start()
        else:
            copy(rz_r.at[n]).start()

    def xo_copy(p):
        return remote(xo.at[p], xw.at[x], snd.at[XO], got.at[XO], {"x": p})

    for i in range(1, 4):
        wz_copy((z + i) % 4).start()
    for d in (3, 0):
        xr_copy(d).start()
    direct(0)
    send_x((3, 0))
    direct(1)
    for i in (1, 3, 2):
        xx_copy((x + i) % 4).start()
    gather_x((3, 0), (0,))
    pass_x((3, 0))
    pass_on(0)
    direct(2)
    gather_x((3, 0), (1, 3))
    pass_on(1)
    direct(3)
    gather_x((3, 0), (2,))
    with jax.named_scope("relay_wait"):
        relay(0, 0).wait_recv()
    with jax.named_scope("product"):
        product(0, (3, 0))

    @pl.when(z == 0)
    def _():
        send_right(0, 3)

    @pl.when(z == 3)
    def _():
        send_left(0, 0, 3)

    pass_on(2)
    direct(4)
    for d in (2, 1):
        xr_copy(d).start()
    send_x((2, 1))
    direct(5)
    gather_x((2, 1), (0,))

    lf[outer] = jnp.zeros((8, TOK), F32)

    @pl.loop(0, NC + 3 * LAG)
    def _(s):
        @pl.when((s >= 1) & (s + 2 < NC))
        def _():
            pass_on(s + 2)

        @pl.when((s >= 1) & (s + 5 < NC))
        def _():
            direct(s + 5)

        @pl.when(s == LAG)
        def _():
            gather_x((2, 1), (1, 3))
            gather_x((2, 1), (2,))

        @pl.when(s == 1)
        def _():
            with jax.named_scope("wz_wait"):
                arrived(wy.at[pl.ds(0, 3), 0], got.at[WZ])

        @pl.when((s >= 11) & (s < 15))
        def _():
            for way in range(2):
                wd_copy(way, s - 11).start()

        for way in range(2):
            @pl.when((s >= 14) & (s < 18) & (s % 2 == way))
            def _():
                j = s - 14
                with jax.named_scope("wd_wait"):
                    arrived(wy.at[j, pl.ds(0, 2)], wd_r.at[j])
                wr_copy(j, way).start()

        @pl.when(s == NC + 4)
        def _():
            with jax.named_scope("wr_wait"):
                arrived(wy.at[:, 2], got.at[WR])
            wc_copy().start()

        @pl.when((s >= 1) & (s < NC))
        def _():
            with jax.named_scope("relay_wait"):
                relay(s, 0).wait_recv()
            with jax.named_scope("product"):
                product(s, (3, 0))

        @pl.when((s >= LAG) & (s < NC + LAG))
        def _():
            with jax.named_scope("product"):
                product(s - LAG, (2, 1))

        for h in (3, 2, 1):
            n = s - LAG * (3 - h)
            ready = (n >= 0) & (n < NC)
            if h == 3:
                ready = ready & (n > 0)

            @pl.when(ready & (z + h < 4))
            def _():
                send_right(n, z + h)

            @pl.when(ready & (z - h >= 0))
            def _():
                send_left(n, z - h, h)

        @pl.when(s == 1)
        def _():
            pass_x((2, 1))

        @pl.when(s >= 3 * LAG)
        def _():
            n = s - 3 * LAG
            mg[n] = pf[n, z]

            @pl.when(z > 0)
            def _():
                with jax.named_scope("last_wait"):
                    remote(sb.at[n, z], rl.at[n, z], snd.at[RS], rs_r.at[n, z], {"z": z_up}).wait_recv()
                mg[n] = mg[n] + rl[n, z].astype(F32)

            @pl.when(z < 3)
            def _():
                with jax.named_scope("last_wait"):
                    remote(sb.at[n, z], rr.at[n, z], snd.at[RS], rz_r.at[n], {"z": z_down}).wait_recv()
                mg[n] = mg[n] + rr[n, z].astype(F32)

            with jax.named_scope("merge"):
                m = mg[n] * (1.0 / TOK) + eb[n]
                mg[n] = m
                lf[outer] = lf[outer] + lax.dot_general(
                    bb[n], m, (((1,), (1,)), ((), ())), precision=lax.Precision.HIGHEST, preferred_element_type=F32
                )

    def lf_copy(i, own):
        o = OUTER_PEERS[i]
        return remote(lf.at[own], lf.at[own], snd.at[LF], got.at[LF], outer_dev(o))

    for i in range(15):
        lf_copy(i, outer).start()

    with jax.named_scope("xx_wait"):
        arrived(xx.at[pl.ds(0, 3)], got.at[XX])
    with jax.named_scope("wc_wait"):
        wc_copy().wait_recv()
    with jax.named_scope("inputs_weight"):
        for h, half in ((core, wy), (1 - core, wo)):
            acc = jnp.zeros((512, SW), F32)
            for j in range(4):
                left = jnp.concatenate([xx[:, ((y + k) % 4) * 4 + j].reshape(512, TOK) for k in range(4)], axis=1)
                acc = acc + jnp.dot(left, half[j].reshape(512, SW), preferred_element_type=F32)
            xo[:, h] = acc.reshape(4, TOK, SW).astype(BF16)
    xw[x] = xo[x]

    with jax.named_scope("lf_wait"):
        arrived(lf.at[pl.ds(0, 15)], got.at[LF])

    with jax.named_scope("gram_schmidt"):
        v = jnp.sum(lf[...], axis=0) * (1.0 / 16)
        rows = lax.broadcasted_iota(jnp.int32, (8, TOK), 0)
        for k in range(8):
            row = v[k:k + 1]
            dots = jnp.sum(v * row, axis=-1, keepdims=True)
            norm = jnp.sqrt(dots[k:k + 1] + 1.0)
            unit = row / norm
            v = jnp.where(rows > k, v - (dots / norm) * unit, jnp.where(rows == k, unit, v))
        lall[c] = v

    def la_copy(i, own):
        return remote(lall.at[own], lall.at[own], snd.at[LA], got.at[LA], chip_dev(CHIP_PEERS[i]))

    with jax.named_scope("right_product"):
        vh = v.astype(BF16)
        for n in range(NC):
            rt[n // 2, :, pl.ds((n % 2) * CW, CW)] = jnp.dot(
                vh, mg[n].astype(BF16), preferred_element_type=F32
            ).astype(BF16)

    def rt_copy(i, to, own):
        return remote(rt.at[to % 8], rsb.at[own], snd.at[RT], got.at[RT], outer_dev(OUTER_PEERS[i]))

    for i in range(15):
        rt_copy(i, outer_at(OUTER_PEERS[i]), outer).start()

    rsb[outer] = rt[sl]

    with jax.named_scope("rt_wait"):
        arrived(rsb.at[pl.ds(0, 15)], got.at[RT])

    rall[c, sl] = (jnp.sum(rsb[...].astype(F32), axis=0) * (1.0 / 16)).astype(BF16)

    def ro_copy(i, own, sem):
        return remote(rall.at[c, own], rall.at[c, own], snd.at[RO], got.at[sem], outer_dev(OUTER_PEERS[i]))

    for i in range(8, 15):
        hands_on = outer_dev(OUTER_PEERS[i])["core"] == x // 2

        @pl.when(hands_on)
        def _():
            ro_copy(i, sl, RO).start()

        @pl.when(jnp.logical_not(hands_on))
        def _():
            ro_copy(i, sl, RO2).start()
    for i in (1, 3, 2):
        xo_copy((x + i) % 4).start()
    for i in range(15):
        la_copy(i, c).start()

    def half_of(k):
        return pl.ds(k * 4, 4)

    def rc_copy(i, own):
        part = rall.at[own, half_of(core)]
        return remote(part, part, snd.at[RC], rc_r.at[own], chip_dev(CHIP_PEERS[i]))

    def rd_copy(own, k):
        part = rall.at[own, half_of(k)]
        return remote(part, part, snd.at[RD], got.at[RD], {"core": 1 - core})

    def ro_wait(sem, with_own):
        with jax.named_scope("ro_wait"):
            @pl.when(with_own)
            def _():
                arrived(rall.at[c, pl.ds(0, 3)], got.at[sem])

            @pl.when(jnp.logical_not(with_own))
            def _():
                arrived(rall.at[c, pl.ds(0, 4)], got.at[sem])

    ro_wait(RO, x // 2 == core)
    for i in range(15):
        rc_copy(i, c).start()
    ro_wait(RO2, x // 2 != core)

    with jax.named_scope("new_error"):
        vt = v.T
        vt_hi = vt.astype(BF16)
        vt_lo = (vt - vt_hi.astype(F32)).astype(BF16)
        for n in range(NC):
            rn = rall[c, n // 2, :, pl.ds((n % 2) * CW, CW)]
            approx = jnp.dot(vt_hi, rn, preferred_element_type=F32) + jnp.dot(vt_lo, rn, preferred_element_type=F32)
            mg[n] = mg[n] - approx
            pltpu.make_async_copy(mg.at[n], ne_hbm.at[0, :, pl.ds(n * CW, CW)], snd.at[NE]).start()

    with jax.named_scope("la_wait"):
        arrived(lall.at[pl.ds(0, 15)], got.at[LA])

    with jax.named_scope("inputs_left"):
        lmat = lall[...].reshape(TOK, TOK)
        lrow = lax.broadcasted_iota(jnp.int32, (TOK, TOK), 0) // 8
        t = jnp.zeros((TOK, TOK), F32)
        for q in range(4):
            lq = jnp.concatenate(
                [jnp.where(lrow == q * 4 + j, lmat, 0.0).astype(BF16) for j in range(4)], axis=1
            )
            xq = jnp.concatenate([xx[x, q * 4 + j] for j in range(4)], axis=1)
            t = t + lax.dot_general(xq, lq, (((1,), (1,)), ((), ())), preferred_element_type=F32)
        t = (t * (-LEARNING_RATE)).astype(BF16)

    with jax.named_scope("rc_wait"):
        for i in reversed(range(15)):
            p = chip_at(CHIP_PEERS[i])
            rc_copy(i, p).wait_recv()
            rd_copy(p, core).start()
    with jax.named_scope("rd_wait"):
        arrived(rall.at[pl.ds(0, 15), pl.ds(0, 4)], got.at[RD])

    with jax.named_scope("xo_wait"):
        arrived(xo.at[pl.ds(0, 3)], got.at[XO])

    with jax.named_scope("outputs"):
        for n in range(NS):
            rn = rall[:, n].astype(F32).reshape(TOK, SW).astype(BF16)
            ob[n] = (xw[n // 2, n % 2].astype(F32) + jnp.dot(t, rn, preferred_element_type=F32)).astype(BF16)
            pltpu.make_async_copy(ob.at[n], out_hbm.at[:, pl.ds(n * SW, SW)], snd.at[OUT]).start()

    with jax.named_scope("drain"):
        for kind, ref in (
            (WZ, wy.at[pl.ds(0, 3), 0]),
            (WD, wy.at[:, pl.ds(0, 2)]),
            (WR, wy.at[:, 0]),
            (WC, wy),
            (XP, xp.at[pl.ds(0, 2)]),
            (XR, xr),
            (XF, xr),
            (XX, xx.at[pl.ds(0, 3)]),
            (DY, dyb.at[:, pl.ds(0, 2)]),
            (RE, dyb.at[:, 0]),
            (RS, sb.at[:, pl.ds(0, 3)]),
            (LF, lf.at[pl.ds(0, 15)]),
            (LA, lall.at[pl.ds(0, 15)]),
            (RT, rsb.at[pl.ds(0, 15)]),
            (RO, rall.at[0, pl.ds(0, 7)]),
            (RC, rall.at[pl.ds(0, 15), pl.ds(0, 4)]),
            (RD, rall.at[pl.ds(0, 15), pl.ds(0, 4)]),
            (XO, xo.at[pl.ds(0, 3)]),
            (NE, mg),
            (OUT, ob),
        ):
            gone(ref, kind)


def step(inputs, out_grads, weight, start_basis, error_buffer):
    vm = pltpu.VMEM
    dma = pltpu.SemaphoreType.DMA
    return pl.pallas_call(
        body,
        out_shape=(
            jax.ShapeDtypeStruct((TOK, D), BF16),
            jax.ShapeDtypeStruct((1, TOK, D), F32),
        ),
        in_specs=[pl.BlockSpec(memory_space=pl.ANY)] * 5,
        out_specs=(pl.BlockSpec(memory_space=pl.ANY),) * 2,
        scratch_shapes=[
            vm((4, 16, TOK, TOK), BF16),
            vm((4, 4, TOK, TOK), BF16),
            vm((4, TOK, TOK), BF16),
            vm((4, TOK, 512), BF16),
            vm((NC, 4, TOK, CW), BF16),
            vm((4, 4, TOK, SW), BF16),
            vm((4, 4, TOK, SW), BF16),
            vm((NC, TOK, CW), F32),
            vm((NC, 8, CW), F32),
            vm((NC, 4, TOK, CW), F32),
            vm((NC, 4, TOK, CW), BF16),
            vm((NC, 4, TOK, CW), BF16),
            vm((NC, 4, TOK, CW), BF16),
            vm((NC, TOK, CW), F32),
            vm((4, 2, TOK, SW), BF16),
            vm((4, 2, TOK, SW), BF16),
            vm((16, 8, TOK), F32),
            vm((16, 8, TOK), F32),
            vm((NS, 8, SW), BF16),
            vm((16, 8, SW), BF16),
            vm((16, NS, 8, SW), BF16),
            vm((NS, TOK, SW), BF16),
            dma((5,)), dma((20,)), dma((20,)), dma((2, 2)), dma((4,)), dma((NC,)), dma((NC,)),
            dma((NC, 4)), dma((NC,)), dma((16,)),
        ],
        compiler_params=pltpu.CompilerParams(
            collective_id=0, has_side_effects=True, vmem_limit_bytes=60 * 1024 * 1024
        ),
    )(inputs, out_grads, weight, start_basis, error_buffer)


def solution(mesh):
    finer = Mesh(mesh.devices.reshape(2, 4, 2, 4, 4), AXES)
    outer = ("zh", "x", "core")
    chip = ("y", "z")
    in_specs = (
        P(outer + chip, None),
        P(outer + chip, None),
        P(chip, None),
        P(chip, None),
        P(outer, chip, None),
    )
    out_specs = (P(outer + chip, None), P(outer, chip, None))
    return jax.shard_map(step, mesh=finer, in_specs=in_specs, out_specs=out_specs, check_vma=False)
```

time: 559 us -> 95.3 us (0.17)
  waiting for transfers between devices: 423 us -> 0 us
  Pallas kernels: 0 us -> 91.5 us
  other arithmetic: 53.3 us -> 0 us
  blocking collectives: 37.2 us -> 0 us
  matrix products: 22.5 us -> 0 us
  between operations: 19.3 us -> 0.65 us
    reduce_scatter x2 -> x0, waiting for transfers between devices: 238 us -> none  [summed_rows(): subtotal = lax.psum_scatter(subtotal, axis, scatter_dimension=0, tiled=True)]
    all_gather x1 -> x0, waiting for transfers between devices: 185 us -> none  [shards(): lax.all_gather(new_weight, CHIP, axis=0, tiled=True)]
    pallas_call x0 -> x1, Pallas kernels: none -> 91.5 us  [step(): pl.pallas_call(body, out_shape=(jax.ShapeDtypeStruct((TOK, D), BF16), jax...]
    all_to_all x2 -> x0, blocking collectives: 37.2 us -> none  [copy_for_each(): lax.all_to_all(jnp.broadcast_to(shard[None], (length, *shard.shape)), axi...]
    reduce_sum x17 -> x0, other arithmetic: 35.7 us -> none  [the longest x11 29.4 us: orthonormal(): vector = vector - jnp.sum(vector * unit, axis=-1, keepdims=True) * unit]
    dot_general x5 -> x0, matrix products: 22.5 us -> none  [the longest x1 9.13 us: shards(): lax.dot_general(columns, out_grads, (((0,), (0,)), ((), ())), preferred_e...]
    div x2 -> x0, other arithmetic: 17.6 us -> none  [the longest x1 17.6 us: orthonormal(): vector / jnp.sqrt(jnp.sum(vector * vector, axis=-1, keepdims=True) + 1.0)]
  transfers between devices with their start and end apart: 3 -> 0, of which waited for: 3 -> 0; matrix products, arithmetic and copies ran while one was open for 0% -> 0% of each run, Pallas kernels for 0% -> 0%
where the time goes in v2:
time: 95.3 us; the launch traced here: 95.1 us
  Pallas kernels  91.5 us (96%)
  local copies, waits for them, and re-layouts  2.94 us (3%)
    pallas_call x1, Pallas kernels, step(): pl.pallas_call(body, out_shape=(jax.ShapeDtypeStruct((TOK, D), BF16), jax...  91.5 us
    unnamed x4, local copies, waits for them, and re-layouts  2.94 us

profile of v2, /device:TPU:1, one launch (start us, length us, event | category | flops | bytes accessed | tf_op | source)
XLA Modules:
  0.0 95.1 jit_solution(15522850028785628937)
XLA Ops:
  0.6 91.5 %shard_map.68 = (bf16[128,2048]{1,0:T(8,128)(2,1)}, f32[1,128,2048]{2,1,0:T(8,128)}) custom-call(bf16[128,2048]{1,0:T(8,128)(2,1)} %x_hbm.1, bf16[128,2048]{1,0:T(8,128)(2,1)} %g_hbm.1, bf16[128,2048]{1,0:T(8,128)(2,1)} %w_hbm.1, f32[8,2048]{1,0:T(8,128)} %b_hbm.1, f32[1,128,2048]{2,1,0:T(8,128)} %e_hbm.1), custom_call_target="tpu_custom_call" | custom-call | tf_op jit(solution)/shard_map/pallas_call | solution.py:507
  92.1 0.0 copy-start
  92.1 2.0 %copy.9 = bf16[128,2048]{1,0:T(8,128)(2,1)} copy(bf16[128,2048]{1,0:T(8,128)(2,1)} %get-tuple-element.4) | data formatting | bytes 1048576
  94.1 0.0 copy-done
  94.1 1.0 %copy.10 = f32[1,128,2048]{2,1,0:T(8,128)} copy(f32[1,128,2048]{2,1,0:T(8,128)S(1)} %copy-done) | data formatting | bytes 2097152
Async XLA Ops:
  92.1 2.0 %copy-start = (f32[1,128,2048]{2,1,0:T(8,128)S(1)}, f32[1,128,2048]{2,1,0:T(8,128)}, u32[]{:S(2)}) copy-start(f32[1,128,2048]{2,1,0:T(8,128)} %get-tuple-element.5) | copy-start | bytes 3145732

commit v3 on v2

--- a/solution.py
+++ b/solution.py
@@ -17,7 +17,7 @@
 SW = D // NS
 LAG = 2
 WZ, WD, WR, WC, XP, XR, XF, XX, DY, RE, RS, LF, LA, RT, RO, RC, RD, XO, NE, OUT = range(20)
-XR2, RO2 = 18, 19
+RO2 = 18
 OUTER_PEERS = [(h, i, k) for h in (1, 0) for i in (2, 1, 3, 0) for k in (0, 1) if (h, i, k) != (0, 0, 0)]
 CHIP_PEERS = [(j, k) for j in (2, 1, 3, 0) for k in (3, 1, 2, 0) if (j, k) != (0, 0)]
 F32 = jnp.float32
@@ -27,7 +27,7 @@
 def body(
     x_hbm, g_hbm, w_hbm, b_hbm, e_hbm, out_hbm, ne_hbm,
     xx, xp, xr, xgt, dyb, wy, wo, eb, bb, pf, sb, rl, rr, mg, xo, xw, lf, lall, rt, rsb, rall, ob,
-    ld, snd, got, xp_r, wd_r, dy_r, re_r, rs_r, rz_r, rc_r,
+    ld, snd, got, xp_r, xr_r, wd_r, dy_r, re_r, rs_r, rz_r, rc_r,
 ):
     zh, x, core, y, z = (lax.axis_index(a) for a in AXES)
     outer = (zh * 4 + x) * 2 + core
@@ -57,7 +57,19 @@
     ring = ((y + 1) % 4, (y + 3) % 4)
     y2 = (y + 2) % 4
     near = (3, 1)
+    goal = (3 - 3 * (z // 2), 2 - z // 2, z + 1 - 2 * (z % 2), z)
     z_up, z_down = (z + 1) % 4, (z + 3) % 4
+
+    def x_load(q, sem):
+        return pltpu.make_async_copy(x_hbm.at[:, pl.ds(pl.multiple_of(q * TOK, TOK), TOK)], xx.at[x, q], ld.at[sem])
+
+    def g_load(n, sem):
+        return pltpu.make_async_copy(g_hbm.at[:, pl.ds(n * CW, CW)], dyb.at[n, 0], ld.at[sem])
+
+    for k in range(4):
+        x_load(k * 4 + goal[0], 0).start()
+    for n in range(2):
+        g_load(n, 1).start()
 
     barrier = pltpu.get_barrier_semaphore()
     for dev in OUTER_PEERS:
@@ -65,18 +77,13 @@
     for dev in CHIP_PEERS:
         pl.semaphore_signal(barrier, inc=1, device_id=chip_dev(dev), device_id_type=MESH_ID)
 
-    w_ld = pltpu.make_async_copy(w_hbm.at[:, pl.ds(pl.multiple_of(sl * SW, SW), SW)], wy.at[z, 0], ld.at[0])
+    for g in (1, 2, 3):
+        for k in range(4):
+            x_load(k * 4 + goal[g], 2).start()
+    for n in range(2, NC):
+        g_load(n, 3).start()
+    w_ld = pltpu.make_async_copy(w_hbm.at[:, pl.ds(pl.multiple_of(sl * SW, SW), SW)], wy.at[z, 0], ld.at[4])
     w_ld.start()
-    x_ld = [pltpu.make_async_copy(x_hbm.at[:, pl.ds(q * TOK, TOK)], xx.at[x, q], ld.at[1]) for q in range(16)]
-    for q in (3, 0, 7, 4, 11, 8, 15, 12, 2, 1, 6, 5, 10, 9, 14, 13):
-        x_ld[q].start()
-    g_ld = [pltpu.make_async_copy(g_hbm.at[:, pl.ds(n * CW, CW)], dyb.at[n, 0], ld.at[2]) for n in range(NC)]
-    for cp in g_ld:
-        cp.start()
-    b_ld = [pltpu.make_async_copy(b_hbm.at[:, pl.ds(n * CW, CW)], bb.at[n], ld.at[3]) for n in range(NC)]
-    e_ld = [pltpu.make_async_copy(e_hbm.at[0, :, pl.ds(n * CW, CW)], eb.at[n], ld.at[4]) for n in range(NC)]
-    for cp in b_ld + e_ld:
-        cp.start()
 
     def arrived(ref, sem):
         remote(ref, ref, snd.at[0], sem, {"core": 1 - core}).wait_recv()
@@ -84,9 +91,8 @@
     def gone(ref, kind):
         remote(ref, ref, snd.at[kind], got.at[0], {"core": 1 - core}).wait_send()
 
-    w_ld.wait()
-    for i, ref in enumerate((xx.at[x], dyb.at[:, 0], bb, eb)):
-        arrived(ref, ld.at[1 + i])
+    arrived(xx.at[x, pl.ds(0, 4)], ld.at[0])
+    arrived(dyb.at[pl.ds(0, 2), 0], ld.at[1])
     with jax.named_scope("entry_barrier"):
         pl.semaphore_wait(barrier, 30)
 
@@ -102,17 +108,18 @@
     def wc_copy():
         return remote(wy, wo, snd.at[WC], got.at[WC], {"core": 1 - core})
 
-    def xp_copy(way, d):
+    def xp_copy(way, g):
         p = ring[way]
-        return remote(xx.at[x, p * 4 + d], xp.at[near[way], d], snd.at[XP], xp_r.at[0, int(d % 3 > 0)], {"y": p})
-
-    def xr_copy(d):
-        way = 0 if d >= 2 else 1
-        return remote(xx.at[x, y2 * 4 + d], xr.at[d], snd.at[XR], got.at[XR2 if d % 3 else XR], {"y": ring[way]})
-
-    def xf_copy(d):
-        way = 0 if d >= 2 else 1
-        return remote(xr.at[d], xp.at[2, d], snd.at[XF], xp_r.at[1, int(d % 3 > 0)], {"y": ring[way]})
+        return remote(xx.at[x, p * 4 + goal[g]], xp.at[near[way], g], snd.at[XP], xp_r.at[0, g], {"y": p})
+
+    def xr_copy(g):
+        return remote(xx.at[x, y2 * 4 + goal[g]], xr.at[g], snd.at[XR], xr_r.at[g], {"y": ring[g % 2]})
+
+    def far_x():
+        return remote(xx.at[x, y2 * 4 + goal[0]], xp.at[2, 0], snd.at[XR], xp_r.at[1, 0], {"y": y2})
+
+    def xf_copy(g):
+        return remote(xr.at[g], xp.at[2, g], snd.at[XF], xp_r.at[1, g], {"y": ring[g % 2]})
 
     def xx_copy(p):
         return remote(xx.at[x], xx.at[x], snd.at[XX], got.at[XX], {"x": p})
@@ -135,31 +142,27 @@
             def _():
                 relay(n, way).start()
 
-    def send_x(ds):
-        for d in ds:
-            for way in range(2):
-                xp_copy(way, d).start()
-
-    def pass_x(ds):
+    def send_x(g):
+        for way in range(2):
+            xp_copy(way, g).start()
+
+    def pass_x(g):
         with jax.named_scope("xr_wait"):
-            arrived(xr.at[pl.ds(0, 2)], got.at[XR2 if ds[0] % 3 else XR])
-        for d in ds:
-            xf_copy(d).start()
-
-    def gather_x(ds, slots):
-        far = int(slots == (2,))
-        if slots != (0,):
-            with jax.named_scope("xp_wait"):
-                arrived(xr.at[pl.ds(0, 2 if far else 4)], xp_r.at[far, int(ds[0] % 3 > 0)])
+            xr_copy(g).wait_recv()
+        xf_copy(g).start()
+
+    def gather_x(g, slots):
+        with jax.named_scope("xp_wait"):
+            if slots == (1, 3):
+                arrived(xr.at[pl.ds(0, 2)], xp_r.at[0, g])
+            if slots == (2,):
+                arrived(xr.at[0], xp_r.at[1, g])
         for k in slots:
-            for d in ds:
-                piece = xp[k, d] if k else xx[x, y * 4 + d]
-                xgt[d, :, pl.ds(k * TOK, TOK)] = piece.T
-
-    def product(n, ds):
-        block = dyb[n].reshape(4 * TOK, CW)
-        for d in ds:
-            pf[n, d] = jnp.dot(xgt[d], block, preferred_element_type=F32)
+            piece = xp[k, g] if k else xx[x, y * 4 + goal[g]]
+            xgt[g, :, pl.ds(k * TOK, TOK)] = piece.T
+
+    def product(n, g):
+        return jnp.dot(xgt[g], dyb[n].reshape(4 * TOK, CW), preferred_element_type=F32)
 
     def send_right(n, d):
         cp = remote(sb.at[n, d], rl.at[n, d], snd.at[RS], rs_r.at[n, d], {"z": z_up})
@@ -199,27 +202,35 @@
     def xo_copy(p):
         return remote(xo.at[p], xw.at[x], snd.at[XO], got.at[XO], {"x": p})
 
+    far_x().start()
+    direct(0)
+    send_x(0)
+    direct(1)
+    arrived(xx.at[x, pl.ds(0, 12)], ld.at[2])
+    xr_copy(1).start()
+    w_ld.wait()
     for i in range(1, 4):
         wz_copy((z + i) % 4).start()
-    for d in (3, 0):
-        xr_copy(d).start()
-    direct(0)
-    send_x((3, 0))
-    direct(1)
     for i in (1, 3, 2):
         xx_copy((x + i) % 4).start()
-    gather_x((3, 0), (0,))
-    pass_x((3, 0))
+    arrived(dyb.at[pl.ds(0, NC - 2), 0], ld.at[3])
+    for n in range(NC):
+        pltpu.make_async_copy(b_hbm.at[:, pl.ds(n * CW, CW)], bb.at[n], ld.at[5]).start()
+        pltpu.make_async_copy(e_hbm.at[0, :, pl.ds(n * CW, CW)], eb.at[n], ld.at[6]).start()
+    gather_x(0, (0,))
     pass_on(0)
     direct(2)
-    gather_x((3, 0), (1, 3))
+    send_x(1)
+    direct(3)
+    gather_x(0, (1, 3))
     pass_on(1)
-    direct(3)
-    gather_x((3, 0), (2,))
+    pass_x(1)
+    direct(4)
+    gather_x(0, (2,))
     with jax.named_scope("relay_wait"):
         relay(0, 0).wait_recv()
     with jax.named_scope("product"):
-        product(0, (3, 0))
+        pf[0, goal[0]] = product(0, 0)
 
     @pl.when(z == 0)
     def _():
@@ -229,14 +240,14 @@
     def _():
         send_left(0, 0, 3)
 
+    xr_copy(2).start()
     pass_on(2)
-    direct(4)
-    for d in (2, 1):
-        xr_copy(d).start()
-    send_x((2, 1))
+    send_x(2)
     direct(5)
-    gather_x((2, 1), (0,))
-
+    gather_x(1, (0,))
+
+    arrived(bb, ld.at[5])
+    arrived(eb, ld.at[6])
     lf[outer] = jnp.zeros((8, TOK), F32)
 
     @pl.loop(0, NC + 3 * LAG)
@@ -249,10 +260,11 @@
         def _():
             direct(s + 5)
 
-        @pl.when(s == LAG)
-        def _():
-            gather_x((2, 1), (1, 3))
-            gather_x((2, 1), (2,))
+        for g in (1, 2, 3):
+            @pl.when(s == LAG * g)
+            def _():
+                gather_x(g, (1, 3))
+                gather_x(g, (2,))
 
         @pl.when(s == 1)
         def _():
@@ -283,12 +295,13 @@
             with jax.named_scope("relay_wait"):
                 relay(s, 0).wait_recv()
             with jax.named_scope("product"):
-                product(s, (3, 0))
-
-        @pl.when((s >= LAG) & (s < NC + LAG))
-        def _():
-            with jax.named_scope("product"):
-                product(s - LAG, (2, 1))
+                pf[s, goal[0]] = product(s, 0)
+
+        for g in (1, 2):
+            @pl.when((s >= LAG * g) & (s < NC + LAG * g))
+            def _():
+                with jax.named_scope("product"):
+                    pf[s - LAG * g, goal[g]] = product(s - LAG * g, g)
 
         for h in (3, 2, 1):
             n = s - LAG * (3 - h)
@@ -306,12 +319,20 @@
 
         @pl.when(s == 1)
         def _():
-            pass_x((2, 1))
+            pass_x(2)
+            xr_copy(3).start()
+            send_x(3)
+            gather_x(2, (0,))
+
+        @pl.when(s == 3)
+        def _():
+            pass_x(3)
+            gather_x(3, (0,))
 
         @pl.when(s >= 3 * LAG)
         def _():
             n = s - 3 * LAG
-            mg[n] = pf[n, z]
+            mg[n] = product(n, 3)
 
             @pl.when(z > 0)
             def _():
@@ -483,7 +504,7 @@
             (WC, wy),
             (XP, xp.at[pl.ds(0, 2)]),
             (XR, xr),
-            (XF, xr),
+            (XF, xr.at[pl.ds(0, 3)]),
             (XX, xx.at[pl.ds(0, 3)]),
             (DY, dyb.at[:, pl.ds(0, 2)]),
             (RE, dyb.at[:, 0]),
@@ -535,7 +556,7 @@
             vm((16, 8, SW), BF16),
             vm((16, NS, 8, SW), BF16),
             vm((NS, TOK, SW), BF16),
-            dma((5,)), dma((20,)), dma((20,)), dma((2, 2)), dma((4,)), dma((NC,)), dma((NC,)),
+            dma((7,)), dma((20,)), dma((20,)), dma((2, 4)), dma((4,)), dma((4,)), dma((NC,)), dma((NC,)),
             dma((NC, 4)), dma((NC,)), dma((16,)),
         ],
         compiler_params=pltpu.CompilerParams(

time: 95.3 us -> 92.5 us (0.971)
  Pallas kernels: 91.5 us -> 88.7 us
    pallas_call x1, Pallas kernels: 91.5 us -> 88.7 us  [step(): pl.pallas_call(body, out_shape=(jax.ShapeDtypeStruct((TOK, D), BF16), jax...]
where the time goes in v3:
time: 92.5 us; the launch traced here: 92.3 us
  Pallas kernels  88.7 us (96%)
  local copies, waits for them, and re-layouts  2.94 us (3%)
    pallas_call x1, Pallas kernels, step(): pl.pallas_call(body, out_shape=(jax.ShapeDtypeStruct((TOK, D), BF16), jax...  88.7 us
    unnamed x4, local copies, waits for them, and re-layouts  2.94 us

profile of v3, /device:TPU:1, one launch (start us, length us, event | category | flops | bytes accessed | tf_op | source)
XLA Modules:
  0.0 92.3 jit_solution(16329247460637617490)
XLA Ops:
  0.6 88.7 %shard_map.68 = (bf16[128,2048]{1,0:T(8,128)(2,1)}, f32[1,128,2048]{2,1,0:T(8,128)}) custom-call(bf16[128,2048]{1,0:T(8,128)(2,1)} %x_hbm.1, bf16[128,2048]{1,0:T(8,128)(2,1)} %g_hbm.1, bf16[128,2048]{1,0:T(8,128)(2,1)} %w_hbm.1, f32[8,2048]{1,0:T(8,128)} %b_hbm.1, f32[1,128,2048]{2,1,0:T(8,128)} %e_hbm.1), custom_call_target="tpu_custom_call" | custom-call | tf_op jit(solution)/shard_map/pallas_call | solution.py:528
  89.4 0.0 copy-start
  89.4 2.0 %copy.9 = bf16[128,2048]{1,0:T(8,128)(2,1)} copy(bf16[128,2048]{1,0:T(8,128)(2,1)} %get-tuple-element.4) | data formatting | bytes 1048576
  91.4 0.0 copy-done
  91.4 1.0 %copy.10 = f32[1,128,2048]{2,1,0:T(8,128)} copy(f32[1,128,2048]{2,1,0:T(8,128)S(1)} %copy-done) | data formatting | bytes 2097152
Async XLA Ops:
  89.4 2.0 %copy-start = (f32[1,128,2048]{2,1,0:T(8,128)S(1)}, f32[1,128,2048]{2,1,0:T(8,128)}, u32[]{:S(2)}) copy-start(f32[1,128,2048]{2,1,0:T(8,128)} %get-tuple-element.5) | copy-start | bytes 3145732

commit v4 on v3

--- a/solution.py
+++ b/solution.py
@@ -15,7 +15,8 @@
 CW = D // NC
 NS = 8
 SW = D // NS
-LAG = 2
+LAGS = (2, 3)
+EARLY = 6
 WZ, WD, WR, WC, XP, XR, XF, XX, DY, RE, RS, LF, LA, RT, RO, RC, RD, XO, NE, OUT = range(20)
 RO2 = 18
 OUTER_PEERS = [(h, i, k) for h in (1, 0) for i in (2, 1, 3, 0) for k in (0, 1) if (h, i, k) != (0, 0, 0)]
@@ -250,7 +251,7 @@
     arrived(eb, ld.at[6])
     lf[outer] = jnp.zeros((8, TOK), F32)
 
-    @pl.loop(0, NC + 3 * LAG)
+    @pl.loop(0, NC + 3 * LAGS[1])
     def _(s):
         @pl.when((s >= 1) & (s + 2 < NC))
         def _():
@@ -261,7 +262,7 @@
             direct(s + 5)
 
         for g in (1, 2, 3):
-            @pl.when(s == LAG * g)
+            @pl.when(s == LAGS[0] * g)
             def _():
                 gather_x(g, (1, 3))
                 gather_x(g, (2,))
@@ -297,15 +298,21 @@
             with jax.named_scope("product"):
                 pf[s, goal[0]] = product(s, 0)
 
+        def turn(k):
+            first, later = s - LAGS[0] * k, s - LAGS[1] * k
+            n = jnp.where(first < EARLY, first, later)
+            return n, (n >= 0) & (n < NC) & ((first < EARLY) | (later >= EARLY))
+
         for g in (1, 2):
-            @pl.when((s >= LAG * g) & (s < NC + LAG * g))
+            n, ready = turn(g)
+
+            @pl.when(ready)
             def _():
                 with jax.named_scope("product"):
-                    pf[s - LAG * g, goal[g]] = product(s - LAG * g, g)
+                    pf[n, goal[g]] = product(n, g)
 
         for h in (3, 2, 1):
-            n = s - LAG * (3 - h)
-            ready = (n >= 0) & (n < NC)
+            n, ready = turn(3 - h)
             if h == 3:
                 ready = ready & (n > 0)
 
@@ -320,18 +327,26 @@
         @pl.when(s == 1)
         def _():
             pass_x(2)
+            gather_x(2, (0,))
+
+        @pl.when(s == 2)
+        def _():
             xr_copy(3).start()
+
+        @pl.when(s == 3)
+        def _():
             send_x(3)
-            gather_x(2, (0,))
-
-        @pl.when(s == 3)
+            gather_x(3, (0,))
+
+        @pl.when(s == 4)
         def _():
             pass_x(3)
-            gather_x(3, (0,))
-
-        @pl.when(s >= 3 * LAG)
-        def _():
-            n = s - 3 * LAG
+
+        last, ready = turn(3)
+
+        @pl.when(ready)
+        def _():
+            n = last
             mg[n] = product(n, 3)
 
             @pl.when(z > 0)
@@ -484,17 +499,23 @@
             p = chip_at(CHIP_PEERS[i])
             rc_copy(i, p).wait_recv()
             rd_copy(p, core).start()
+    with jax.named_scope("xo_wait"):
+        arrived(xo.at[pl.ds(0, 3)], got.at[XO])
+
+    def finish(first):
+        for k in range(4):
+            n = first + k
+            rn = rall[:, n].astype(F32).reshape(TOK, SW).astype(BF16)
+            ob[n] = (xw[n // 2, n % 2].astype(F32) + jnp.dot(t, rn, preferred_element_type=F32)).astype(BF16)
+            columns = pl.ds(pl.multiple_of(n * SW, SW), SW)
+            pltpu.make_async_copy(ob.at[n], out_hbm.at[:, columns], snd.at[OUT]).start()
+
+    with jax.named_scope("outputs"):
+        finish(core * 4)
     with jax.named_scope("rd_wait"):
         arrived(rall.at[pl.ds(0, 15), pl.ds(0, 4)], got.at[RD])
-
-    with jax.named_scope("xo_wait"):
-        arrived(xo.at[pl.ds(0, 3)], got.at[XO])
-
     with jax.named_scope("outputs"):
-        for n in range(NS):
-            rn = rall[:, n].astype(F32).reshape(TOK, SW).astype(BF16)
-            ob[n] = (xw[n // 2, n % 2].astype(F32) + jnp.dot(t, rn, preferred_element_type=F32)).astype(BF16)
-            pltpu.make_async_copy(ob.at[n], out_hbm.at[:, pl.ds(n * SW, SW)], snd.at[OUT]).start()
+        finish(4 - core * 4)
 
     with jax.named_scope("drain"):
         for kind, ref in (

time: 92.5 us -> 91.5 us (0.989)
  Pallas kernels: 88.7 us -> 87.7 us
    pallas_call x1, Pallas kernels: 88.7 us -> 87.7 us  [step(): pl.pallas_call(body, out_shape=(jax.ShapeDtypeStruct((TOK, D), BF16), jax...]
where the time goes in v4:
time: 91.5 us; the launch traced here: 91.3 us
  Pallas kernels  87.7 us (96%)
  local copies, waits for them, and re-layouts  2.94 us (3%)
    pallas_call x1, Pallas kernels, step(): pl.pallas_call(body, out_shape=(jax.ShapeDtypeStruct((TOK, D), BF16), jax...  87.7 us
    unnamed x4, local copies, waits for them, and re-layouts  2.94 us

profile of v4, /device:TPU:1, one launch (start us, length us, event | category | flops | bytes accessed | tf_op | source)
XLA Modules:
  0.0 91.3 jit_solution(7939053463954193483)
XLA Ops:
  0.6 87.7 %shard_map.68 = (bf16[128,2048]{1,0:T(8,128)(2,1)}, f32[1,128,2048]{2,1,0:T(8,128)}) custom-call(bf16[128,2048]{1,0:T(8,128)(2,1)} %x_hbm.1, bf16[128,2048]{1,0:T(8,128)(2,1)} %g_hbm.1, bf16[128,2048]{1,0:T(8,128)(2,1)} %w_hbm.1, f32[8,2048]{1,0:T(8,128)} %b_hbm.1, f32[1,128,2048]{2,1,0:T(8,128)} %e_hbm.1), custom_call_target="tpu_custom_call" | custom-call | tf_op jit(solution)/shard_map/pallas_call | solution.py:549
  88.3 0.0 copy-start
  88.3 2.0 %copy.9 = bf16[128,2048]{1,0:T(8,128)(2,1)} copy(bf16[128,2048]{1,0:T(8,128)(2,1)} %get-tuple-element.4) | data formatting | bytes 1048576
  90.3 0.0 copy-done
  90.3 1.0 %copy.10 = f32[1,128,2048]{2,1,0:T(8,128)} copy(f32[1,128,2048]{2,1,0:T(8,128)S(1)} %copy-done) | data formatting | bytes 2097152
Async XLA Ops:
  88.3 2.0 %copy-start = (f32[1,128,2048]{2,1,0:T(8,128)S(1)}, f32[1,128,2048]{2,1,0:T(8,128)}, u32[]{:S(2)}) copy-start(f32[1,128,2048]{2,1,0:T(8,128)} %get-tuple-element.5) | copy-start | bytes 3145732

commit v5 on v4

--- a/solution.py
+++ b/solution.py
@@ -397,9 +397,9 @@
         for k in range(8):
             row = v[k:k + 1]
             dots = jnp.sum(v * row, axis=-1, keepdims=True)
-            norm = jnp.sqrt(dots[k:k + 1] + 1.0)
-            unit = row / norm
-            v = jnp.where(rows > k, v - (dots / norm) * unit, jnp.where(rows == k, unit, v))
+            square = dots[k:k + 1] + 1.0
+            unit = row / jnp.sqrt(square)
+            v = jnp.where(rows > k, v - (dots / square) * row, jnp.where(rows == k, unit, v))
         lall[c] = v
 
     def la_copy(i, own):
@@ -423,61 +423,59 @@
     with jax.named_scope("rt_wait"):
         arrived(rsb.at[pl.ds(0, 15)], got.at[RT])
 
-    rall[c, sl] = (jnp.sum(rsb[...].astype(F32), axis=0) * (1.0 / 16)).astype(BF16)
-
-    def ro_copy(i, own, sem):
-        return remote(rall.at[c, own], rall.at[c, own], snd.at[RO], got.at[sem], outer_dev(OUTER_PEERS[i]))
+    rall[c, core, 0] = (jnp.sum(rsb[...].astype(F32), axis=0) * (1.0 / 16)).astype(BF16)
+
+    def ro_copy(i):
+        _, step, other = OUTER_PEERS[i]
+        return remote(
+            rall.at[c, core, 0], rall.at[c, core, (4 - step) % 4],
+            snd.at[RO], got.at[RO2 if other else RO], outer_dev(OUTER_PEERS[i]),
+        )
 
     for i in range(8, 15):
-        hands_on = outer_dev(OUTER_PEERS[i])["core"] == x // 2
-
-        @pl.when(hands_on)
-        def _():
-            ro_copy(i, sl, RO).start()
-
-        @pl.when(jnp.logical_not(hands_on))
-        def _():
-            ro_copy(i, sl, RO2).start()
+        ro_copy(i).start()
+
+    def first_copy(i):
+        part = rall.at[c, core, 0]
+        return remote(part, part, snd.at[RC], got.at[RC], chip_dev(CHIP_PEERS[i]))
+
+    for i in range(15):
+        first_copy(i).start()
     for i in (1, 3, 2):
         xo_copy((x + i) % 4).start()
     for i in range(15):
         la_copy(i, c).start()
 
-    def half_of(k):
-        return pl.ds(k * 4, 4)
-
     def rc_copy(i, own):
-        part = rall.at[own, half_of(core)]
+        part = rall.at[own, core, pl.ds(1, 3)]
         return remote(part, part, snd.at[RC], rc_r.at[own], chip_dev(CHIP_PEERS[i]))
 
-    def rd_copy(own, k):
-        part = rall.at[own, half_of(k)]
+    def rd_copy(own):
+        part = rall.at[own, core]
         return remote(part, part, snd.at[RD], got.at[RD], {"core": 1 - core})
 
-    def ro_wait(sem, with_own):
-        with jax.named_scope("ro_wait"):
-            @pl.when(with_own)
-            def _():
-                arrived(rall.at[c, pl.ds(0, 3)], got.at[sem])
-
-            @pl.when(jnp.logical_not(with_own))
-            def _():
-                arrived(rall.at[c, pl.ds(0, 4)], got.at[sem])
-
-    ro_wait(RO, x // 2 == core)
+    with jax.named_scope("ro_wait"):
+        arrived(rall.at[c, 0, pl.ds(0, 3)], got.at[RO])
     for i in range(15):
         rc_copy(i, c).start()
-    ro_wait(RO2, x // 2 != core)
+    with jax.named_scope("ro_wait"):
+        arrived(rall.at[c, 0], got.at[RO2])
 
     with jax.named_scope("new_error"):
         vt = v.T
         vt_hi = vt.astype(BF16)
         vt_lo = (vt - vt_hi.astype(F32)).astype(BF16)
-        for n in range(NC):
-            rn = rall[c, n // 2, :, pl.ds((n % 2) * CW, CW)]
-            approx = jnp.dot(vt_hi, rn, preferred_element_type=F32) + jnp.dot(vt_lo, rn, preferred_element_type=F32)
-            mg[n] = mg[n] - approx
-            pltpu.make_async_copy(mg.at[n], ne_hbm.at[0, :, pl.ds(n * CW, CW)], snd.at[NE]).start()
+        for i in range(2):
+            for r in range(4):
+                for half in range(2):
+                    n = (((x + r) % 4) * 2 + i) * 2 + half
+                    rn = rall[c, i, r, :, pl.ds(half * CW, CW)]
+                    approx = jnp.dot(vt_hi, rn, preferred_element_type=F32) + jnp.dot(
+                        vt_lo, rn, preferred_element_type=F32
+                    )
+                    mg[n] = mg[n] - approx
+                    columns = pl.ds(pl.multiple_of(n * CW, CW), CW)
+                    pltpu.make_async_copy(mg.at[n], ne_hbm.at[0, :, columns], snd.at[NE]).start()
 
     with jax.named_scope("la_wait"):
         arrived(lall.at[pl.ds(0, 15)], got.at[LA])
@@ -495,27 +493,28 @@
         t = (t * (-LEARNING_RATE)).astype(BF16)
 
     with jax.named_scope("rc_wait"):
+        arrived(rall.at[pl.ds(0, 15), 0, 0], got.at[RC])
         for i in reversed(range(15)):
             p = chip_at(CHIP_PEERS[i])
             rc_copy(i, p).wait_recv()
-            rd_copy(p, core).start()
+            rd_copy(p).start()
     with jax.named_scope("xo_wait"):
         arrived(xo.at[pl.ds(0, 3)], got.at[XO])
 
-    def finish(first):
-        for k in range(4):
-            n = first + k
-            rn = rall[:, n].astype(F32).reshape(TOK, SW).astype(BF16)
-            ob[n] = (xw[n // 2, n % 2].astype(F32) + jnp.dot(t, rn, preferred_element_type=F32)).astype(BF16)
+    def finish(i):
+        for r in range(4):
+            n = ((x + r) % 4) * 2 + i
+            rn = rall[:, i, r].astype(F32).reshape(TOK, SW).astype(BF16)
+            ob[n] = (xw[(x + r) % 4, i].astype(F32) + jnp.dot(t, rn, preferred_element_type=F32)).astype(BF16)
             columns = pl.ds(pl.multiple_of(n * SW, SW), SW)
             pltpu.make_async_copy(ob.at[n], out_hbm.at[:, columns], snd.at[OUT]).start()
 
     with jax.named_scope("outputs"):
-        finish(core * 4)
+        finish(core)
     with jax.named_scope("rd_wait"):
-        arrived(rall.at[pl.ds(0, 15), pl.ds(0, 4)], got.at[RD])
+        arrived(rall.at[pl.ds(0, 15), 0], got.at[RD])
     with jax.named_scope("outputs"):
-        finish(4 - core * 4)
+        finish(1 - core)
 
     with jax.named_scope("drain"):
         for kind, ref in (
@@ -533,9 +532,9 @@
             (LF, lf.at[pl.ds(0, 15)]),
             (LA, lall.at[pl.ds(0, 15)]),
             (RT, rsb.at[pl.ds(0, 15)]),
-            (RO, rall.at[0, pl.ds(0, 7)]),
-            (RC, rall.at[pl.ds(0, 15), pl.ds(0, 4)]),
-            (RD, rall.at[pl.ds(0, 15), pl.ds(0, 4)]),
+            (RO, rall.at[pl.ds(0, 7), 0, 0]),
+            (RC, rall.at[pl.ds(0, 15), 0]),
+            (RD, rall.at[pl.ds(0, 15), 0]),
             (XO, xo.at[pl.ds(0, 3)]),
             (NE, mg),
             (OUT, ob),
@@ -575,7 +574,7 @@
             vm((16, 8, TOK), F32),
             vm((NS, 8, SW), BF16),
             vm((16, 8, SW), BF16),
-            vm((16, NS, 8, SW), BF16),
+            vm((16, 2, 4, 8, SW), BF16),
             vm((NS, TOK, SW), BF16),
             dma((7,)), dma((20,)), dma((20,)), dma((2, 4)), dma((4,)), dma((4,)), dma((NC,)), dma((NC,)),
             dma((NC, 4)), dma((NC,)), dma((16,)),

time: 91.5 us -> 90.6 us (level)
  no operation moved by 1% of the time
where the time goes in v5:
time: 90.6 us; the launch traced here: 90.4 us
  Pallas kernels  86.8 us (96%)
  local copies, waits for them, and re-layouts  2.94 us (3%)
    pallas_call x1, Pallas kernels, step(): pl.pallas_call(body, out_shape=(jax.ShapeDtypeStruct((TOK, D), BF16), jax...  86.8 us
    unnamed x4, local copies, waits for them, and re-layouts  2.94 us

profile of v5, /device:TPU:1, one launch (start us, length us, event | category | flops | bytes accessed | tf_op | source)
XLA Modules:
  0.0 90.4 jit_solution(15281493439644051916)
XLA Ops:
  0.6 86.8 %shard_map.68 = (bf16[128,2048]{1,0:T(8,128)(2,1)}, f32[1,128,2048]{2,1,0:T(8,128)}) custom-call(bf16[128,2048]{1,0:T(8,128)(2,1)} %x_hbm.1, bf16[128,2048]{1,0:T(8,128)(2,1)} %g_hbm.1, bf16[128,2048]{1,0:T(8,128)(2,1)} %w_hbm.1, f32[8,2048]{1,0:T(8,128)} %b_hbm.1, f32[1,128,2048]{2,1,0:T(8,128)} %e_hbm.1), custom_call_target="tpu_custom_call" | custom-call | tf_op jit(solution)/shard_map/pallas_call | solution.py:548
  87.4 0.0 copy-start
  87.4 2.0 %copy.9 = bf16[128,2048]{1,0:T(8,128)(2,1)} copy(bf16[128,2048]{1,0:T(8,128)(2,1)} %get-tuple-element.4) | data formatting | bytes 1048576
  89.4 0.0 copy-done
  89.4 1.0 %copy.10 = f32[1,128,2048]{2,1,0:T(8,128)} copy(f32[1,128,2048]{2,1,0:T(8,128)S(1)} %copy-done) | data formatting | bytes 2097152
Async XLA Ops:
  87.4 2.0 %copy-start = (f32[1,128,2048]{2,1,0:T(8,128)S(1)}, f32[1,128,2048]{2,1,0:T(8,128)}, u32[]{:S(2)}) copy-start(f32[1,128,2048]{2,1,0:T(8,128)} %get-tuple-element.5) | copy-start | bytes 3145732

commit v6 on v5

--- a/solution.py
+++ b/solution.py
@@ -17,6 +17,7 @@
 SW = D // NS
 LAGS = (2, 3)
 EARLY = 6
+SEMS = 12
 WZ, WD, WR, WC, XP, XR, XF, XX, DY, RE, RS, LF, LA, RT, RO, RC, RD, XO, NE, OUT = range(20)
 RO2 = 18
 OUTER_PEERS = [(h, i, k) for h in (1, 0) for i in (2, 1, 3, 0) for k in (0, 1) if (h, i, k) != (0, 0, 0)]
@@ -126,10 +127,10 @@
         return remote(xx.at[x], xx.at[x], snd.at[XX], got.at[XX], {"x": p})
 
     def dy_copy(way, n):
-        return remote(dyb.at[n, 0], dyb.at[n, near[way]], snd.at[DY], dy_r.at[n], {"y": ring[way]})
+        return remote(dyb.at[n, 0], dyb.at[n, near[way]], snd.at[DY], dy_r.at[n % SEMS], {"y": ring[way]})
 
     def relay(n, way):
-        return remote(dyb.at[n, near[way]], dyb.at[n, 2], snd.at[RE], re_r.at[n], {"y": ring[way]})
+        return remote(dyb.at[n, near[way]], dyb.at[n, 2], snd.at[RE], re_r.at[n % SEMS], {"y": ring[way]})
 
     def direct(n):
         for way in range(2):
@@ -137,7 +138,7 @@
 
     def pass_on(n):
         with jax.named_scope("direct_wait"):
-            arrived(dyb.at[n, pl.ds(0, 2)], dy_r.at[n])
+            arrived(dyb.at[n, pl.ds(0, 2)], dy_r.at[n % SEMS])
         for way in range(2):
             @pl.when(n % 2 == way)
             def _():
@@ -166,7 +167,7 @@
         return jnp.dot(xgt[g], dyb[n].reshape(4 * TOK, CW), preferred_element_type=F32)
 
     def send_right(n, d):
-        cp = remote(sb.at[n, d], rl.at[n, d], snd.at[RS], rs_r.at[n, d], {"z": z_up})
+        cp = remote(sb.at[n, d], rl.at[n, d], snd.at[RS], rs_r.at[n % SEMS, d], {"z": z_up})
 
         @pl.when(z == 0)
         def _():
@@ -192,13 +193,13 @@
         @pl.when(z < 3)
         def _():
             with jax.named_scope("left_wait"):
-                copy(rs_r.at[n, d]).wait_recv()
+                copy(rs_r.at[n % SEMS, d]).wait_recv()
             sb[n, d] = (pf[n, d] + rr[n, d].astype(F32)).astype(BF16)
 
         if h > 1:
-            copy(rs_r.at[n, d]).start()
+            copy(rs_r.at[n % SEMS, d]).start()
         else:
-            copy(rz_r.at[n]).start()
+            copy(rz_r.at[n % SEMS]).start()
 
     def xo_copy(p):
         return remote(xo.at[p], xw.at[x], snd.at[XO], got.at[XO], {"x": p})
@@ -352,13 +353,13 @@
             @pl.when(z > 0)
             def _():
                 with jax.named_scope("last_wait"):
-                    remote(sb.at[n, z], rl.at[n, z], snd.at[RS], rs_r.at[n, z], {"z": z_up}).wait_recv()
+                    remote(sb.at[n, z], rl.at[n, z], snd.at[RS], rs_r.at[n % SEMS, z], {"z": z_up}).wait_recv()
                 mg[n] = mg[n] + rl[n, z].astype(F32)
 
             @pl.when(z < 3)
             def _():
                 with jax.named_scope("last_wait"):
-                    remote(sb.at[n, z], rr.at[n, z], snd.at[RS], rz_r.at[n], {"z": z_down}).wait_recv()
+                    remote(sb.at[n, z], rr.at[n, z], snd.at[RS], rz_r.at[n % SEMS], {"z": z_down}).wait_recv()
                 mg[n] = mg[n] + rr[n, z].astype(F32)
 
             with jax.named_scope("merge"):
@@ -576,8 +577,8 @@
             vm((16, 8, SW), BF16),
             vm((16, 2, 4, 8, SW), BF16),
             vm((NS, TOK, SW), BF16),
-            dma((7,)), dma((20,)), dma((20,)), dma((2, 4)), dma((4,)), dma((4,)), dma((NC,)), dma((NC,)),
-            dma((NC, 4)), dma((NC,)), dma((16,)),
+            dma((7,)), dma((20,)), dma((20,)), dma((2, 4)), dma((4,)), dma((4,)), dma((SEMS,)), dma((SEMS,)),
+            dma((SEMS, 4)), dma((SEMS,)), dma((16,)),
         ],
         compiler_params=pltpu.CompilerParams(
             collective_id=0, has_side_effects=True, vmem_limit_bytes=60 * 1024 * 1024

time: 90.6 us -> 90.3 us (level)
  no operation moved by 1% of the time
where the time goes in v6:
time: 90.3 us; the launch traced here: 90.2 us
  Pallas kernels  86.6 us (96%)
  local copies, waits for them, and re-layouts  2.94 us (3%)
    pallas_call x1, Pallas kernels, step(): pl.pallas_call(body, out_shape=(jax.ShapeDtypeStruct((TOK, D), BF16), jax...  86.6 us
    unnamed x4, local copies, waits for them, and re-layouts  2.94 us

profile of v6, /device:TPU:1, one launch (start us, length us, event | category | flops | bytes accessed | tf_op | source)
XLA Modules:
  0.0 90.2 jit_solution(2679683136913312021)
XLA Ops:
  0.6 86.6 %shard_map.68 = (bf16[128,2048]{1,0:T(8,128)(2,1)}, f32[1,128,2048]{2,1,0:T(8,128)}) custom-call(bf16[128,2048]{1,0:T(8,128)(2,1)} %x_hbm.1, bf16[128,2048]{1,0:T(8,128)(2,1)} %g_hbm.1, bf16[128,2048]{1,0:T(8,128)(2,1)} %w_hbm.1, f32[8,2048]{1,0:T(8,128)} %b_hbm.1, f32[1,128,2048]{2,1,0:T(8,128)} %e_hbm.1), custom_call_target="tpu_custom_call" | custom-call | tf_op jit(solution)/shard_map/pallas_call | solution.py:549
  87.2 0.0 copy-start
  87.2 2.0 %copy.9 = bf16[128,2048]{1,0:T(8,128)(2,1)} copy(bf16[128,2048]{1,0:T(8,128)(2,1)} %get-tuple-element.4) | data formatting | bytes 1048576
  89.2 0.0 copy-done
  89.2 1.0 %copy.10 = f32[1,128,2048]{2,1,0:T(8,128)} copy(f32[1,128,2048]{2,1,0:T(8,128)S(1)} %copy-done) | data formatting | bytes 2097152
Async XLA Ops:
  87.2 2.0 %copy-start = (f32[1,128,2048]{2,1,0:T(8,128)S(1)}, f32[1,128,2048]{2,1,0:T(8,128)}, u32[]{:S(2)}) copy-start(f32[1,128,2048]{2,1,0:T(8,128)} %get-tuple-element.5) | copy-start | bytes 3145732
